TPU v7x, 32 devices: a whole 2x2x4 slice. The times are simulated.
32 devices in a mesh: chan: 16 (over z, y, core), wall: 2 (over x).
Axes of the slice: x: 2, y: 2, z: 4, core: 2. Of those that a mesh axis runs over, the one named last changes fastest.
Arguments:
- coords: float32 [3, 16, 2, 4096], P(None, 'chan', 'wall'), as said below
- masses: float32 [16, 2, 4096], P('chan', 'wall'), may hold values from 0.5 to 2
- counts: int32 [16, 2, 16], P('chan', 'wall'), may hold values from 64 to 256
- lists: int32 [16, 2, 5, 16, 2], P('chan', 'wall'), may hold values from 0 to 47, as said below
Outputs:
- density: float32 [16, 2, 4096], P('chan', 'wall')
Inputs may be any that keep to these rules, and one draw needn't show every extreme that they name: `lists`: each row of 2 entries names different tiles; tile t of extended slab s is s * 16 + t, slab 0 the lower cross-wall neighbour, 1 the slab itself, 2 the upper neighbour. `coords`: channel components lie in [0, 1), cross-wall and depth components in [0, 8).
All inputs are finite; a program needn't handle non-finite values.
Results may differ from a plain program's by a relative error of at most 0.0003.
Values sent between devices are 32-bit elements; how exact they have to be, the bound alone decides.
No kernel may reach another device: no remote copies, remote signals or barrier semaphores. Data moves between devices by JAX's collectives and lax.ppermute only.
A program may use at most 64 MiB of HBM per device.

v0:
```python
import math

import jax
import jax.numpy as jnp
from jax import lax
from jax.sharding import PartitionSpec as P

NB = 2
R = 4


def extended_2(block, sides, width):
    for axis, dim in sides:
        count = lax.axis_size(axis)
        forward = [(i, i + 1) for i in range(count - 1)]
        backward = [(target, source) for source, target in forward]
        low = lax.ppermute(
            lax.slice_in_dim(block, block.shape[dim] - width, None, axis=dim), axis, forward
        )
        high = lax.ppermute(lax.slice_in_dim(block, 0, width, axis=dim), axis, backward)
        block = jnp.concatenate([low, block, high], axis=dim)
    return block


def from_behind(block, axis, distance):
    devices = range(lax.axis_size(axis))
    route = [((i - distance) % len(devices), i) for i in devices]
    return lax.ppermute(block, axis, route)


def from_behind_2(block, axis, distance):
    devices = range(lax.axis_size(axis))
    route = [(i - distance, i) for i in devices if i - distance in devices]
    return lax.ppermute(block, axis, route)


def spline(scaled):
    return (jnp.maximum(2.0 - scaled, 0.0) ** 3 * 0.25 - jnp.maximum(1.0 - scaled, 0.0) ** 3) * (
        1.0 / math.pi
    )


def pair_block(own_block, partner, partner_rows, offset, with_back):
    tile_count = own_block.shape[1]
    tile_len = own_block.shape[2]
    list_len = partner_rows.shape[1]
    picked = jnp.take(partner, partner_rows.reshape(-1), axis=1).reshape(
        4, tile_count, list_len, tile_len
    )
    wall_lift = (partner_rows // tile_count - 1).astype(jnp.float32) * (2.0 * R)
    reach = float(R)

    def single_tile(inputs):
        own_tile, theirs, shift_y = inputs
        delta_x = own_tile[0][None, :, None] - (theirs[0][:, None, :] + offset)
        delta_y = own_tile[1][None, :, None] - (theirs[1][:, None, :] + shift_y[:, None, None])
        delta_z = own_tile[2][None, :, None] - theirs[2][:, None, :]
        distance = jnp.sqrt(delta_x * delta_x + delta_y * delta_y + delta_z * delta_z + 0.0001)
        weight = spline(distance / reach)
        gained = jnp.sum(weight * theirs[3][:, None, :], axis=(0, 2))
        handed = jnp.sum(weight * own_tile[3][None, :, None], axis=1)
        return (gained, handed)

    group = math.gcd(tile_count, 4)

    def grouped(values):
        return values.reshape((tile_count // group, group) + values.shape[1:])

    gained, handed = lax.map(
        jax.vmap(single_tile),
        (
            grouped(jnp.moveaxis(own_block, 1, 0)),
            grouped(jnp.moveaxis(picked, 1, 0)),
            grouped(wall_lift),
        ),
    )
    gained = gained.reshape(tile_count, tile_len)
    handed = handed.reshape(tile_count, list_len, tile_len)
    if not with_back:
        return (gained, None)
    onehot = (
        partner_rows.reshape(-1)[:, None] == jnp.arange(partner.shape[1], dtype=jnp.int32)[None, :]
    ).astype(jnp.float32)
    returned = jnp.dot(onehot.T, handed.reshape(-1, tile_len), precision=lax.Precision.HIGHEST)
    return (gained, returned)


def on_device(coords, masses, counts, lists):
    tile_count = counts.shape[2]
    tile_len = masses.shape[2] // tile_count
    slots = jnp.arange(tile_len, dtype=jnp.int32)
    filled = (slots[None, :] < counts[0, 0][:, None]).astype(jnp.float32)
    weighted = masses.reshape(tile_count, tile_len) * filled
    packed = jnp.concatenate([coords, weighted.reshape(1, 1, 1, -1)], axis=0)
    extended = extended_2(packed, (("wall", 2),), 1)
    extended = extended.reshape(4, 3 * tile_count, tile_len)
    own_block = packed.reshape(4, tile_count, tile_len)
    partner_rows = lists[0, 0]
    density, unused_back = pair_block(own_block, extended, partner_rows[0], 0.0, False)
    returns = jnp.zeros((3 * tile_count, tile_len), jnp.float32)
    for step in range(1, R + 1):
        partner = from_behind(extended, "chan", -step)
        gained, handed = pair_block(own_block, partner, partner_rows[step], float(step), True)
        density = density + gained
        returns = returns + from_behind(handed, "chan", step)
    from_below = from_behind_2(returns[2 * tile_count :], "wall", 1)
    from_above = from_behind_2(returns[:tile_count], "wall", -1)
    total = density + returns[tile_count : 2 * tile_count] + from_below + from_above
    return (total * filled / (NB * tile_len)).reshape(1, 1, -1)


def solution(mesh):
    placed = (
        P(None, "chan", "wall", None),
        P("chan", "wall", None),
        P("chan", "wall", None),
        P("chan", "wall", None, None, None),
    )
    return jax.shard_map(
        on_device, mesh=mesh, in_specs=placed, out_specs=P("chan", "wall", None), check_vma=False
    )
```

profile of v0, /device:TPU:0, one launch (start us, length us, event | category | flops | bytes accessed | tf_op | source)
XLA Modules:
  0.0 103.7 jit_solution(12260350591247521337)
XLA Ops:
  0.0 0.8 iota_compare_fusion.4
  0.8 0.7 bitcast_select_fusion
  1.6 0.9 pad_maximum_fusion.2
  2.4 4.9 %collective-permute-start = (f32[4,1,1,4096]{3,2,1,0:T(1,128)S(1)}, f32[4,1,1,4096]{3,2,1,0:T(1,128)S(1)}, u32[]{:S(2)}, u32[]{:S(2)}) collective-permute-start(f32[4,1,1,4096]{3,2,1,0:T(1,128)S(1)} %pad_maximum_fusion.2), channel_id=1, source_target_pairs={{0,1},{2,3},{4,5},{6,7},{8,9},{10,11},{12,13},{14,15},{16,17},{18,... | collective-permute-start | bytes 196616 | tf_op jit(solution)/shard_map/ppermute | solution.py:17
  7.3 1.3 %collective-permute-start.1 = (f32[4,1,1,4096]{3,2,1,0:T(1,128)S(1)}, f32[4,1,1,4096]{3,2,1,0:T(1,128)S(1)}, u32[]{:S(2)}, u32[]{:S(2)}) collective-permute-start(f32[4,1,1,4096]{3,2,1,0:T(1,128)S(1)} %pad_maximum_fusion.2), channel_id=1, source_target_pairs={{1,0},{3,2},{5,4},{7,6},{9,8},{11,10},{13,12},{15,14},{17,16},{19,... | collective-permute-start | bytes 196616 | tf_op jit(solution)/shard_map/ppermute | solution.py:20
  8.6 0.8 fusion.68
  10.9 0.1 reduce
  11.3 2.2 %collective-permute-done.1 = f32[4,1,1,4096]{3,2,1,0:T(1,128)S(1)} collective-permute-done((f32[4,1,1,4096]{3,2,1,0:T(1,128)S(1)}, f32[4,1,1,4096]{3,2,1,0:T(1,128)S(1)}, u32[]{:S(2)}, u32[]{:S(2)}) %collective-permute-start.1) | collective-permute-done | bytes 65568 | tf_op jit(solution)/shard_map/ppermute | solution.py:20
  13.5 0.2 pad_maximum_fusion
  13.7 0.1 reshape.315
  13.8 0.1 copy.104
  14.0 1.7 %collective-permute-start.4 = (f32[4,48,256]{2,0,1:T(4,128)S(1)}, f32[4,48,256]{2,0,1:T(4,128)S(1)}, u32[]{:S(2)}, u32[]{:S(2)}) collective-permute-start(f32[4,48,256]{2,0,1:T(4,128)S(1)} %copy.104), channel_id=1, source_target_pairs={{6,0},{8,2},{10,4},{12,6},{14,8},{16,10},{18,12},{20,14},{22,16},{... | collective-permute-start | bytes 589832 | tf_op jit(solution)/shard_map/ppermute | solution.py:28
  15.6 3.0 %collective-permute-start.3 = (f32[4,48,256]{2,0,1:T(4,128)S(1)}, f32[4,48,256]{2,0,1:T(4,128)S(1)}, u32[]{:S(2)}, u32[]{:S(2)}) collective-permute-start(f32[4,48,256]{2,0,1:T(4,128)S(1)} %copy.104), channel_id=1, source_target_pairs={{4,0},{6,2},{8,4},{10,6},{12,8},{14,10},{16,12},{18,14},{20,16},{2... | collective-permute-start | bytes 589832 | tf_op jit(solution)/shard_map/ppermute | solution.py:28
  18.6 1.3 %collective-permute-start.2 = (f32[4,48,256]{2,0,1:T(4,128)S(1)}, f32[4,48,256]{2,0,1:T(4,128)S(1)}, u32[]{:S(2)}, u32[]{:S(2)}) collective-permute-start(f32[4,48,256]{2,0,1:T(4,128)S(1)} %copy.104), channel_id=1, source_target_pairs={{2,0},{4,2},{6,4},{8,6},{10,8},{12,10},{14,12},{16,14},{18,16},{20... | collective-permute-start | bytes 589832 | tf_op jit(solution)/shard_map/ppermute | solution.py:28
  19.9 0.4 collective-permute-start.5
  20.4 0.6 gather_fusion
  21.0 0.1 broadcast_select_fusion.4
  21.1 0.6 gather_fusion.3
  21.8 0.1 broadcast_select_fusion.1
  21.9 12.6 %while.61 = (s32[]{:T(128)}, f32[4,4,256]{2,1,0:T(4,128)S(1)}, f32[4,4,2,256]{3,2,1,0:T(2,128)S(1)}, f32[4,4,4,256]{3,1,2,0:T(4,128)S(1)}, f32[4,4,4,2,256]{4,2,...) while((s32[]{:T(128)}, f32[4,4,256]{2,1,0:T(4,128)S(1)}, f32[4,4,2,256]{3,2,1,0:T(2,128)S(1)}, ...), condition=%wide.region_14.16_spmd, body=%wide.region_11.15_spmd.sunk | while | flops 12587010 | bytes 348417 | solution.py:69
  22.0 0.1 copy.165
  22.2 2.8 %multiply_reduce_fusion.14 = (f32[4,2,256]{2,1,0:T(2,128)S(1)}, f32[4,256]{1,0:T(4,128)S(1)}) fusion(f32[4,256]{1,0:T(4,128)S(1)} %get-tuple-element.665, f32[4,2,256]{2,1,0:T(2,128)S(1)} %get-tuple-element.666, f32[4,256]{1,0:T(4,128)S(1)} %get-tuple-element.667, f32[4,2,256]{2,1,0:T(2,128)S(1)} %fusion.90, f32[4,256]{1,0:T(4,128)S(1)} %get-tuple-element.668, ...), kind=kLoop, calls=%fused_computation.77.clone.1 | loop fusion | flops 12579840 | bytes 61440 | tf_op jit(solution)/shard_map/while/body/eval_jaxpr/vmap()/reduce_sum | solution.py:61
  25.1 0.1 copy.165
  25.3 2.8 %multiply_reduce_fusion.14 = (f32[4,2,256]{2,1,0:T(2,128)S(1)}, f32[4,256]{1,0:T(4,128)S(1)}) fusion(f32[4,256]{1,0:T(4,128)S(1)} %get-tuple-element.665, f32[4,2,256]{2,1,0:T(2,128)S(1)} %get-tuple-element.666, f32[4,256]{1,0:T(4,128)S(1)} %get-tuple-element.667, f32[4,2,256]{2,1,0:T(2,128)S(1)} %fusion.90, f32[4,256]{1,0:T(4,128)S(1)} %get-tuple-element.668, ...), kind=kLoop, calls=%fused_computation.77.clone.1 | loop fusion | flops 12579840 | bytes 61440 | tf_op jit(solution)/shard_map/while/body/eval_jaxpr/vmap()/reduce_sum | solution.py:61
  28.5 2.8 %multiply_reduce_fusion.14 = (f32[4,2,256]{2,1,0:T(2,128)S(1)}, f32[4,256]{1,0:T(4,128)S(1)}) fusion(f32[4,256]{1,0:T(4,128)S(1)} %get-tuple-element.665, f32[4,2,256]{2,1,0:T(2,128)S(1)} %get-tuple-element.666, f32[4,256]{1,0:T(4,128)S(1)} %get-tuple-element.667, f32[4,2,256]{2,1,0:T(2,128)S(1)} %fusion.90, f32[4,256]{1,0:T(4,128)S(1)} %get-tuple-element.668, ...), kind=kLoop, calls=%fused_computation.77.clone.1 | loop fusion | flops 12579840 | bytes 61440 | tf_op jit(solution)/shard_map/while/body/eval_jaxpr/vmap()/reduce_sum | solution.py:61
  31.6 2.8 %multiply_reduce_fusion.14 = (f32[4,2,256]{2,1,0:T(2,128)S(1)}, f32[4,256]{1,0:T(4,128)S(1)}) fusion(f32[4,256]{1,0:T(4,128)S(1)} %get-tuple-element.665, f32[4,2,256]{2,1,0:T(2,128)S(1)} %get-tuple-element.666, f32[4,256]{1,0:T(4,128)S(1)} %get-tuple-element.667, f32[4,2,256]{2,1,0:T(2,128)S(1)} %fusion.90, f32[4,256]{1,0:T(4,128)S(1)} %get-tuple-element.668, ...), kind=kLoop, calls=%fused_computation.77.clone.1 | loop fusion | flops 12579840 | bytes 61440 | tf_op jit(solution)/shard_map/while/body/eval_jaxpr/vmap()/reduce_sum | solution.py:61
  34.5 0.6 gather_fusion.2
  35.1 0.1 broadcast_select_fusion.2
  35.2 12.6 %while.60 = (s32[]{:T(128)}, f32[4,4,256]{2,1,0:T(4,128)S(1)}, f32[4,4,2,256]{3,2,1,0:T(2,128)S(1)}, f32[4,4,4,256]{3,1,2,0:T(4,128)S(1)}, f32[4,4,4,2,256]{4,2,...) while((s32[]{:T(128)}, f32[4,4,256]{2,1,0:T(4,128)S(1)}, f32[4,4,2,256]{3,2,1,0:T(2,128)S(1)}, ...), condition=%wide.region_10.12_spmd, body=%wide.region_7.11_spmd.sunk | while | flops 12587010 | bytes 348417 | solution.py:69
  35.5 2.8 %multiply_reduce_fusion.13 = (f32[4,2,256]{2,1,0:T(2,128)S(1)}, f32[4,256]{1,0:T(4,128)S(1)}) fusion(f32[4,256]{1,0:T(4,128)S(1)} %get-tuple-element.650, f32[4,2,256]{2,1,0:T(2,128)S(1)} %get-tuple-element.651, f32[4,256]{1,0:T(4,128)S(1)} %get-tuple-element.652, f32[4,2,256]{2,1,0:T(2,128)S(1)} %fusion.88, f32[4,256]{1,0:T(4,128)S(1)} %get-tuple-element.653, ...), kind=kLoop, calls=%fused_computation.53.clone.1 | loop fusion | flops 12579840 | bytes 61440 | tf_op jit(solution)/shard_map/while/body/eval_jaxpr/vmap()/reduce_sum | solution.py:61
  38.7 2.8 %multiply_reduce_fusion.13 = (f32[4,2,256]{2,1,0:T(2,128)S(1)}, f32[4,256]{1,0:T(4,128)S(1)}) fusion(f32[4,256]{1,0:T(4,128)S(1)} %get-tuple-element.650, f32[4,2,256]{2,1,0:T(2,128)S(1)} %get-tuple-element.651, f32[4,256]{1,0:T(4,128)S(1)} %get-tuple-element.652, f32[4,2,256]{2,1,0:T(2,128)S(1)} %fusion.88, f32[4,256]{1,0:T(4,128)S(1)} %get-tuple-element.653, ...), kind=kLoop, calls=%fused_computation.53.clone.1 | loop fusion | flops 12579840 | bytes 61440 | tf_op jit(solution)/shard_map/while/body/eval_jaxpr/vmap()/reduce_sum | solution.py:61
  41.8 2.8 %multiply_reduce_fusion.13 = (f32[4,2,256]{2,1,0:T(2,128)S(1)}, f32[4,256]{1,0:T(4,128)S(1)}) fusion(f32[4,256]{1,0:T(4,128)S(1)} %get-tuple-element.650, f32[4,2,256]{2,1,0:T(2,128)S(1)} %get-tuple-element.651, f32[4,256]{1,0:T(4,128)S(1)} %get-tuple-element.652, f32[4,2,256]{2,1,0:T(2,128)S(1)} %fusion.88, f32[4,256]{1,0:T(4,128)S(1)} %get-tuple-element.653, ...), kind=kLoop, calls=%fused_computation.53.clone.1 | loop fusion | flops 12579840 | bytes 61440 | tf_op jit(solution)/shard_map/while/body/eval_jaxpr/vmap()/reduce_sum | solution.py:61
  45.0 2.8 %multiply_reduce_fusion.13 = (f32[4,2,256]{2,1,0:T(2,128)S(1)}, f32[4,256]{1,0:T(4,128)S(1)}) fusion(f32[4,256]{1,0:T(4,128)S(1)} %get-tuple-element.650, f32[4,2,256]{2,1,0:T(2,128)S(1)} %get-tuple-element.651, f32[4,256]{1,0:T(4,128)S(1)} %get-tuple-element.652, f32[4,2,256]{2,1,0:T(2,128)S(1)} %fusion.88, f32[4,256]{1,0:T(4,128)S(1)} %get-tuple-element.653, ...), kind=kLoop, calls=%fused_computation.53.clone.1 | loop fusion | flops 12579840 | bytes 61440 | tf_op jit(solution)/shard_map/while/body/eval_jaxpr/vmap()/reduce_sum | solution.py:61
  47.8 0.6 gather_fusion.1
  48.5 0.1 broadcast_select_fusion.3
  48.6 12.6 %while.59 = (s32[]{:T(128)}, f32[4,4,256]{2,1,0:T(4,128)S(1)}, f32[4,4,2,256]{3,2,1,0:T(2,128)S(1)}, f32[4,4,4,256]{3,1,2,0:T(4,128)S(1)}, f32[4,4,4,2,256]{4,2,...) while((s32[]{:T(128)}, f32[4,4,256]{2,1,0:T(4,128)S(1)}, f32[4,4,2,256]{3,2,1,0:T(2,128)S(1)}, ...), condition=%wide.region_6.8_spmd, body=%wide.region_3.7_spmd.sunk | while | flops 12587010 | bytes 348417 | solution.py:69
  48.9 2.8 %multiply_reduce_fusion.12 = (f32[4,2,256]{2,1,0:T(2,128)S(1)}, f32[4,256]{1,0:T(4,128)S(1)}) fusion(f32[4,256]{1,0:T(4,128)S(1)} %get-tuple-element.635, f32[4,2,256]{2,1,0:T(2,128)S(1)} %get-tuple-element.636, f32[4,256]{1,0:T(4,128)S(1)} %get-tuple-element.637, f32[4,2,256]{2,1,0:T(2,128)S(1)} %fusion.86, f32[4,256]{1,0:T(4,128)S(1)} %get-tuple-element.638, ...), kind=kLoop, calls=%fused_computation.29.clone.1 | loop fusion | flops 12579840 | bytes 61440 | tf_op jit(solution)/shard_map/while/body/eval_jaxpr/vmap()/reduce_sum | solution.py:61
  52.0 2.8 %multiply_reduce_fusion.12 = (f32[4,2,256]{2,1,0:T(2,128)S(1)}, f32[4,256]{1,0:T(4,128)S(1)}) fusion(f32[4,256]{1,0:T(4,128)S(1)} %get-tuple-element.635, f32[4,2,256]{2,1,0:T(2,128)S(1)} %get-tuple-element.636, f32[4,256]{1,0:T(4,128)S(1)} %get-tuple-element.637, f32[4,2,256]{2,1,0:T(2,128)S(1)} %fusion.86, f32[4,256]{1,0:T(4,128)S(1)} %get-tuple-element.638, ...), kind=kLoop, calls=%fused_computation.29.clone.1 | loop fusion | flops 12579840 | bytes 61440 | tf_op jit(solution)/shard_map/while/body/eval_jaxpr/vmap()/reduce_sum | solution.py:61
  55.2 2.8 %multiply_reduce_fusion.12 = (f32[4,2,256]{2,1,0:T(2,128)S(1)}, f32[4,256]{1,0:T(4,128)S(1)}) fusion(f32[4,256]{1,0:T(4,128)S(1)} %get-tuple-element.635, f32[4,2,256]{2,1,0:T(2,128)S(1)} %get-tuple-element.636, f32[4,256]{1,0:T(4,128)S(1)} %get-tuple-element.637, f32[4,2,256]{2,1,0:T(2,128)S(1)} %fusion.86, f32[4,256]{1,0:T(4,128)S(1)} %get-tuple-element.638, ...), kind=kLoop, calls=%fused_computation.29.clone.1 | loop fusion | flops 12579840 | bytes 61440 | tf_op jit(solution)/shard_map/while/body/eval_jaxpr/vmap()/reduce_sum | solution.py:61
  58.3 2.8 %multiply_reduce_fusion.12 = (f32[4,2,256]{2,1,0:T(2,128)S(1)}, f32[4,256]{1,0:T(4,128)S(1)}) fusion(f32[4,256]{1,0:T(4,128)S(1)} %get-tuple-element.635, f32[4,2,256]{2,1,0:T(2,128)S(1)} %get-tuple-element.636, f32[4,256]{1,0:T(4,128)S(1)} %get-tuple-element.637, f32[4,2,256]{2,1,0:T(2,128)S(1)} %fusion.86, f32[4,256]{1,0:T(4,128)S(1)} %get-tuple-element.638, ...), kind=kLoop, calls=%fused_computation.29.clone.1 | loop fusion | flops 12579840 | bytes 61440 | tf_op jit(solution)/shard_map/while/body/eval_jaxpr/vmap()/reduce_sum | solution.py:61
  61.2 0.6 gather_fusion.4
  61.8 0.1 broadcast_select_fusion
  62.0 12.6 %while.62 = (s32[]{:T(128)}, f32[4,4,256]{2,1,0:T(4,128)S(1)}, f32[4,4,2,256]{3,2,1,0:T(2,128)S(1)}, f32[4,4,4,256]{3,1,2,0:T(4,128)S(1)}, f32[4,4,4,2,256]{4,2,...) while((s32[]{:T(128)}, f32[4,4,256]{2,1,0:T(4,128)S(1)}, f32[4,4,2,256]{3,2,1,0:T(2,128)S(1)}, ...), condition=%wide.region_18.20_spmd, body=%wide.region_15.19_spmd.sunk | while | flops 12587010 | bytes 348417 | solution.py:69
  62.2 2.8 %multiply_reduce_fusion.15 = (f32[4,2,256]{2,1,0:T(2,128)S(1)}, f32[4,256]{1,0:T(4,128)S(1)}) fusion(f32[4,256]{1,0:T(4,128)S(1)} %get-tuple-element.680, f32[4,2,256]{2,1,0:T(2,128)S(1)} %get-tuple-element.681, f32[4,256]{1,0:T(4,128)S(1)} %get-tuple-element.682, f32[4,2,256]{2,1,0:T(2,128)S(1)} %fusion.92, f32[4,256]{1,0:T(4,128)S(1)} %get-tuple-element.683, ...), kind=kLoop, calls=%fused_computation.101.clone.1 | loop fusion | flops 12579840 | bytes 61440 | tf_op jit(solution)/shard_map/while/body/eval_jaxpr/vmap()/reduce_sum | solution.py:61
  65.4 2.8 %multiply_reduce_fusion.15 = (f32[4,2,256]{2,1,0:T(2,128)S(1)}, f32[4,256]{1,0:T(4,128)S(1)}) fusion(f32[4,256]{1,0:T(4,128)S(1)} %get-tuple-element.680, f32[4,2,256]{2,1,0:T(2,128)S(1)} %get-tuple-element.681, f32[4,256]{1,0:T(4,128)S(1)} %get-tuple-element.682, f32[4,2,256]{2,1,0:T(2,128)S(1)} %fusion.92, f32[4,256]{1,0:T(4,128)S(1)} %get-tuple-element.683, ...), kind=kLoop, calls=%fused_computation.101.clone.1 | loop fusion | flops 12579840 | bytes 61440 | tf_op jit(solution)/shard_map/while/body/eval_jaxpr/vmap()/reduce_sum | solution.py:61
  68.5 2.8 %multiply_reduce_fusion.15 = (f32[4,2,256]{2,1,0:T(2,128)S(1)}, f32[4,256]{1,0:T(4,128)S(1)}) fusion(f32[4,256]{1,0:T(4,128)S(1)} %get-tuple-element.680, f32[4,2,256]{2,1,0:T(2,128)S(1)} %get-tuple-element.681, f32[4,256]{1,0:T(4,128)S(1)} %get-tuple-element.682, f32[4,2,256]{2,1,0:T(2,128)S(1)} %fusion.92, f32[4,256]{1,0:T(4,128)S(1)} %get-tuple-element.683, ...), kind=kLoop, calls=%fused_computation.101.clone.1 | loop fusion | flops 12579840 | bytes 61440 | tf_op jit(solution)/shard_map/while/body/eval_jaxpr/vmap()/reduce_sum | solution.py:61
  71.7 2.8 %multiply_reduce_fusion.15 = (f32[4,2,256]{2,1,0:T(2,128)S(1)}, f32[4,256]{1,0:T(4,128)S(1)}) fusion(f32[4,256]{1,0:T(4,128)S(1)} %get-tuple-element.680, f32[4,2,256]{2,1,0:T(2,128)S(1)} %get-tuple-element.681, f32[4,256]{1,0:T(4,128)S(1)} %get-tuple-element.682, f32[4,2,256]{2,1,0:T(2,128)S(1)} %fusion.92, f32[4,256]{1,0:T(4,128)S(1)} %get-tuple-element.683, ...), kind=kLoop, calls=%fused_computation.101.clone.1 | loop fusion | flops 12579840 | bytes 61440 | tf_op jit(solution)/shard_map/while/body/eval_jaxpr/vmap()/reduce_sum | solution.py:61
  74.5 0.3 fusion.34
  74.8 1.7 %collective-permute-start.6 = (f32[48,256]{1,0:T(8,128)S(1)}, f32[48,256]{1,0:T(8,128)S(1)}, u32[]{:S(2)}, u32[]{:S(2)}) collective-permute-start(f32[48,256]{1,0:T(8,128)S(1)} %fusion.34), channel_id=1, source_target_pairs={{30,0},{0,2},{2,4},{4,6},{6,8},{8,10},{10,12},{12,14},{14,16},{16,... | collective-permute-start | bytes 147464 | tf_op jit(solution)/shard_map/ppermute | solution.py:28
  76.5 0.3 fusion.35
  76.8 0.9 collective-permute-start.7
  77.8 0.3 fusion.36
  78.1 2.5 %collective-permute-start.8 = (f32[48,256]{1,0:T(8,128)S(1)}, f32[48,256]{1,0:T(8,128)S(1)}, u32[]{:S(2)}, u32[]{:S(2)}) collective-permute-start(f32[48,256]{1,0:T(8,128)S(1)} %fusion.36), channel_id=1, source_target_pairs={{26,0},{28,2},{30,4},{0,6},{2,8},{4,10},{6,12},{8,14},{10,16},{12,... | collective-permute-start | bytes 147464 | tf_op jit(solution)/shard_map/ppermute | solution.py:28
  80.6 0.3 fusion.37
  80.9 1.6 %collective-permute-start.9 = (f32[48,256]{1,0:T(8,128)S(1)}, f32[48,256]{1,0:T(8,128)S(1)}, u32[]{:S(2)}, u32[]{:S(2)}) collective-permute-start(f32[48,256]{1,0:T(8,128)S(1)} %fusion.37), channel_id=1, source_target_pairs={{24,0},{26,2},{28,4},{30,6},{0,8},{2,10},{4,12},{6,14},{8,16},{10,... | collective-permute-start | bytes 147464 | tf_op jit(solution)/shard_map/ppermute | solution.py:28
  82.5 12.4 %while.58 = (s32[]{:T(128)}, f32[4,4,256]{2,1,0:T(4,128)S(1)}, f32[4,4,4,256]{3,1,2,0:T(4,128)S(1)}, f32[4,4,4,2,256]{4,2,3,1,0:T(4,128)S(1)}, f32[4,4,2]{1,0,2:T(4,128)S(1)}, /*index=5*/s32[]{:T(128)}) while((s32[]{:T(128)}, f32[4,4,256]{2,1,0:T(4,128)S(1)}, f32[4,4,4,256]{3,1,2,0:T(4,128)S(1)}, f32[4,4,4,2,256]{4,2,3,1,0:T(4,128)S(1)}, ...), condition=%wide.region_2.4_spmd, body=%wide.region_0.3_spmd.sunk | while | flops 11537410 | bytes 311541 | solution.py:69
  82.8 2.8 %fusion.84 = f32[4,256]{1,0:T(4,128)S(1)} fusion(f32[4,2,256]{2,1,0:T(2,128)S(1)} %get-tuple-element.623, f32[4,2,256]{2,1,0:T(2,128)S(1)} %get-tuple-element.624, f32[4,256]{1,0:T(4,128)S(1)} %get-tuple-element.625, f32[4,2,256]{2,1,0:T(2,128)S(1)} %fusion.83, f32[4,256]{1,0:T(4,128)S(1)} %get-tuple-element.626, ...), kind=kLoop, calls=%fused_computation.10.clone.1 | loop fusion | flops 11533312 | bytes 49152 | tf_op jit(solution)/shard_map/while/body/eval_jaxpr/vmap()/reduce_sum | solution.py:60
  85.9 2.8 %fusion.84 = f32[4,256]{1,0:T(4,128)S(1)} fusion(f32[4,2,256]{2,1,0:T(2,128)S(1)} %get-tuple-element.623, f32[4,2,256]{2,1,0:T(2,128)S(1)} %get-tuple-element.624, f32[4,256]{1,0:T(4,128)S(1)} %get-tuple-element.625, f32[4,2,256]{2,1,0:T(2,128)S(1)} %fusion.83, f32[4,256]{1,0:T(4,128)S(1)} %get-tuple-element.626, ...), kind=kLoop, calls=%fused_computation.10.clone.1 | loop fusion | flops 11533312 | bytes 49152 | tf_op jit(solution)/shard_map/while/body/eval_jaxpr/vmap()/reduce_sum | solution.py:60
  89.0 2.8 %fusion.84 = f32[4,256]{1,0:T(4,128)S(1)} fusion(f32[4,2,256]{2,1,0:T(2,128)S(1)} %get-tuple-element.623, f32[4,2,256]{2,1,0:T(2,128)S(1)} %get-tuple-element.624, f32[4,256]{1,0:T(4,128)S(1)} %get-tuple-element.625, f32[4,2,256]{2,1,0:T(2,128)S(1)} %fusion.83, f32[4,256]{1,0:T(4,128)S(1)} %get-tuple-element.626, ...), kind=kLoop, calls=%fused_computation.10.clone.1 | loop fusion | flops 11533312 | bytes 49152 | tf_op jit(solution)/shard_map/while/body/eval_jaxpr/vmap()/reduce_sum | solution.py:60
  92.1 2.8 %fusion.84 = f32[4,256]{1,0:T(4,128)S(1)} fusion(f32[4,2,256]{2,1,0:T(2,128)S(1)} %get-tuple-element.623, f32[4,2,256]{2,1,0:T(2,128)S(1)} %get-tuple-element.624, f32[4,256]{1,0:T(4,128)S(1)} %get-tuple-element.625, f32[4,2,256]{2,1,0:T(2,128)S(1)} %fusion.83, f32[4,256]{1,0:T(4,128)S(1)} %get-tuple-element.626, ...), kind=kLoop, calls=%fused_computation.10.clone.1 | loop fusion | flops 11533312 | bytes 49152 | tf_op jit(solution)/shard_map/while/body/eval_jaxpr/vmap()/reduce_sum | solution.py:60
  95.0 2.3 %collective-permute-start.10 = (f32[16,256]{1,0:T(8,128)S(1)}, f32[16,256]{1,0:T(8,128)S(1)}, u32[]{:S(2)}, u32[]{:S(2)}) collective-permute-start(f32[16,256]{1,0:T(8,128)S(1)} %get-tuple-element.419), channel_id=1, source_target_pairs={{0,1},{2,3},{4,5},{6,7},{8,9},{10,11},{12,13},{14,15},{16,17},{18,... | collective-permute-start | bytes 49160 | tf_op jit(solution)/shard_map/ppermute | solution.py:34
  97.4 1.3 %collective-permute-start.11 = (f32[16,256]{1,0:T(8,128)S(1)}, f32[16,256]{1,0:T(8,128)S(1)}, u32[]{:S(2)}, u32[]{:S(2)}) collective-permute-start(f32[16,256]{1,0:T(8,128)S(1)} %get-tuple-element.420), channel_id=1, source_target_pairs={{1,0},{3,2},{5,4},{7,6},{9,8},{11,10},{13,12},{15,14},{17,16},{19,... | collective-permute-start | bytes 49160 | tf_op jit(solution)/shard_map/ppermute | solution.py:34
  98.8 4.2 %collective-permute-done.11 = f32[16,256]{1,0:T(8,128)S(1)} collective-permute-done((f32[16,256]{1,0:T(8,128)S(1)}, f32[16,256]{1,0:T(8,128)S(1)}, u32[]{:S(2)}, u32[]{:S(2)}) %collective-permute-start.11) | collective-permute-done | bytes 16416 | tf_op jit(solution)/shard_map/ppermute | solution.py:34
  103.1 0.6 reshape.326
  (267 shorter events, 6.9 us)
Async XLA Ops:
  0.0 10.8 %copy-start.2 = (s32[1,1,16]{2,1,0:T(1,128)S(1)}, s32[1,1,16]{2,1,0:T(1,128)}, u32[]{:S(2)}) copy-start(s32[1,1,16]{2,1,0:T(1,128)} %param.18) | copy-start | bytes 196
  0.0 10.8 %copy-start.1 = (f32[1,1,4096]{2,1,0:T(1,128)S(1)}, f32[1,1,4096]{2,1,0:T(1,128)}, u32[]{:S(2)}) copy-start(f32[1,1,4096]{2,1,0:T(1,128)} %param.17) | copy-start | bytes 49156
  0.0 10.9 %copy-start = (f32[3,1,1,4096]{3,2,1,0:T(1,128)S(1)}, f32[3,1,1,4096]{3,2,1,0:T(1,128)}, u32[]{:S(2)}) copy-start(f32[3,1,1,4096]{3,2,1,0:T(1,128)} %param.16) | copy-start | bytes 147460
  2.4 8.8 %collective-permute-start = (f32[4,1,1,4096]{3,2,1,0:T(1,128)S(1)}, f32[4,1,1,4096]{3,2,1,0:T(1,128)S(1)}, u32[]{:S(2)}, u32[]{:S(2)}) collective-permute-start(f32[4,1,1,4096]{3,2,1,0:T(1,128)S(1)} %pad_maximum_fusion.2), channel_id=1, source_target_pairs={{0,1},{2,3},{4,5},{6,7},{8,9},{10,11},{12,13},{14,15},{16,17},{18,... | collective-permute-start | bytes 196616 | tf_op jit(solution)/shard_map/ppermute | solution.py:17
  7.3 6.2 %collective-permute-start.1 = (f32[4,1,1,4096]{3,2,1,0:T(1,128)S(1)}, f32[4,1,1,4096]{3,2,1,0:T(1,128)S(1)}, u32[]{:S(2)}, u32[]{:S(2)}) collective-permute-start(f32[4,1,1,4096]{3,2,1,0:T(1,128)S(1)} %pad_maximum_fusion.2), channel_id=1, source_target_pairs={{1,0},{3,2},{5,4},{7,6},{9,8},{11,10},{13,12},{15,14},{17,16},{19,... | collective-permute-start | bytes 196616 | tf_op jit(solution)/shard_map/ppermute | solution.py:20
  14.0 7.2 %collective-permute-start.4 = (f32[4,48,256]{2,0,1:T(4,128)S(1)}, f32[4,48,256]{2,0,1:T(4,128)S(1)}, u32[]{:S(2)}, u32[]{:S(2)}) collective-permute-start(f32[4,48,256]{2,0,1:T(4,128)S(1)} %copy.104), channel_id=1, source_target_pairs={{6,0},{8,2},{10,4},{12,6},{14,8},{16,10},{18,12},{20,14},{22,16},{... | collective-permute-start | bytes 589832 | tf_op jit(solution)/shard_map/ppermute | solution.py:28
  15.6 18.8 %collective-permute-start.3 = (f32[4,48,256]{2,0,1:T(4,128)S(1)}, f32[4,48,256]{2,0,1:T(4,128)S(1)}, u32[]{:S(2)}, u32[]{:S(2)}) collective-permute-start(f32[4,48,256]{2,0,1:T(4,128)S(1)} %copy.104), channel_id=1, source_target_pairs={{4,0},{6,2},{8,4},{10,6},{12,8},{14,10},{16,12},{18,14},{20,16},{2... | collective-permute-start | bytes 589832 | tf_op jit(solution)/shard_map/ppermute | solution.py:28
  18.6 29.2 %collective-permute-start.2 = (f32[4,48,256]{2,0,1:T(4,128)S(1)}, f32[4,48,256]{2,0,1:T(4,128)S(1)}, u32[]{:S(2)}, u32[]{:S(2)}) collective-permute-start(f32[4,48,256]{2,0,1:T(4,128)S(1)} %copy.104), channel_id=1, source_target_pairs={{2,0},{4,2},{6,4},{8,6},{10,8},{12,10},{14,12},{16,14},{18,16},{20... | collective-permute-start | bytes 589832 | tf_op jit(solution)/shard_map/ppermute | solution.py:28
  19.9 41.2 %collective-permute-start.5 = (f32[4,48,256]{2,0,1:T(4,128)S(1)}, f32[4,48,256]{2,0,1:T(4,128)S(1)}, u32[]{:S(2)}, u32[]{:S(2)}) collective-permute-start(f32[4,48,256]{2,0,1:T(4,128)S(1)} %copy.104), channel_id=1, source_target_pairs={{8,0},{10,2},{12,4},{14,6},{16,8},{18,10},{20,12},{22,14},{24,16},... | collective-permute-start | bytes 589832 | tf_op jit(solution)/shard_map/ppermute | solution.py:28
  74.8 20.1 %collective-permute-start.6 = (f32[48,256]{1,0:T(8,128)S(1)}, f32[48,256]{1,0:T(8,128)S(1)}, u32[]{:S(2)}, u32[]{:S(2)}) collective-permute-start(f32[48,256]{1,0:T(8,128)S(1)} %fusion.34), channel_id=1, source_target_pairs={{30,0},{0,2},{2,4},{4,6},{6,8},{8,10},{10,12},{12,14},{14,16},{16,... | collective-permute-start | bytes 147464 | tf_op jit(solution)/shard_map/ppermute | solution.py:28
  76.8 18.1 %collective-permute-start.7 = (f32[48,256]{1,0:T(8,128)S(1)}, f32[48,256]{1,0:T(8,128)S(1)}, u32[]{:S(2)}, u32[]{:S(2)}) collective-permute-start(f32[48,256]{1,0:T(8,128)S(1)} %fusion.35), channel_id=1, source_target_pairs={{28,0},{30,2},{0,4},{2,6},{4,8},{6,10},{8,12},{10,14},{12,16},{14,... | collective-permute-start | bytes 147464 | tf_op jit(solution)/shard_map/ppermute | solution.py:28
  78.1 16.9 %collective-permute-start.8 = (f32[48,256]{1,0:T(8,128)S(1)}, f32[48,256]{1,0:T(8,128)S(1)}, u32[]{:S(2)}, u32[]{:S(2)}) collective-permute-start(f32[48,256]{1,0:T(8,128)S(1)} %fusion.36), channel_id=1, source_target_pairs={{26,0},{28,2},{30,4},{0,6},{2,8},{4,10},{6,12},{8,14},{10,16},{12,... | collective-permute-start | bytes 147464 | tf_op jit(solution)/shard_map/ppermute | solution.py:28
  80.9 14.1 %collective-permute-start.9 = (f32[48,256]{1,0:T(8,128)S(1)}, f32[48,256]{1,0:T(8,128)S(1)}, u32[]{:S(2)}, u32[]{:S(2)}) collective-permute-start(f32[48,256]{1,0:T(8,128)S(1)} %fusion.37), channel_id=1, source_target_pairs={{24,0},{26,2},{28,4},{30,6},{0,8},{2,10},{4,12},{6,14},{8,16},{10,... | collective-permute-start | bytes 147464 | tf_op jit(solution)/shard_map/ppermute | solution.py:28
  95.0 3.8 %collective-permute-start.10 = (f32[16,256]{1,0:T(8,128)S(1)}, f32[16,256]{1,0:T(8,128)S(1)}, u32[]{:S(2)}, u32[]{:S(2)}) collective-permute-start(f32[16,256]{1,0:T(8,128)S(1)} %get-tuple-element.419), channel_id=1, source_target_pairs={{0,1},{2,3},{4,5},{6,7},{8,9},{10,11},{12,13},{14,15},{16,17},{18,... | collective-permute-start | bytes 49160 | tf_op jit(solution)/shard_map/ppermute | solution.py:34
  97.4 5.6 %collective-permute-start.11 = (f32[16,256]{1,0:T(8,128)S(1)}, f32[16,256]{1,0:T(8,128)S(1)}, u32[]{:S(2)}, u32[]{:S(2)}) collective-permute-start(f32[16,256]{1,0:T(8,128)S(1)} %get-tuple-element.420), channel_id=1, source_target_pairs={{1,0},{3,2},{5,4},{7,6},{9,8},{11,10},{13,12},{15,14},{17,16},{19,... | collective-permute-start | bytes 49160 | tf_op jit(solution)/shard_map/ppermute | solution.py:34
where the time goes:
time: 104 us
  other arithmetic  61.6 us (59%)
  starting transfers between devices  23 us (22%)
  local copies, waits for them, and re-layouts  9.6 us (9%)
  waiting for transfers between devices  6.55 us (6%)
  loops' own time  1.3 us (1%)
  matrix products  1.15 us (1%)
    reduce_sum x16, other arithmetic, single_tile(): handed = jnp.sum(weight * own_tile[3][None, :, None], axis=1)  45 us
    ppermute x8, starting transfers between devices, from_behind(): return lax.ppermute(block, axis, route)  13.2 us
    reduce_sum x4, other arithmetic, single_tile(): gained = jnp.sum(weight * theirs[3][:, None, :], axis=(0, 2))  11.2 us
    ppermute x1, starting transfers between devices, extended_2(): lax.ppermute(lax.slice_in_dim(block, block.shape[dim] - width, None, axis...  4.87 us
    ppermute x2, waiting for transfers between devices, from_behind_2(): return lax.ppermute(block, axis, route)  4.3 us
    ppermute x2, starting transfers between devices, from_behind_2(): return lax.ppermute(block, axis, route)  3.63 us
    gather x5, local copies, waits for them, and re-layouts, pair_block(): jnp.take(partner, partner_rows.reshape(-1), axis=1)  3.16 us
    ppermute x1, waiting for transfers between devices, extended_2(): lax.ppermute(lax.slice_in_dim(block, 0, width, axis=dim), axis, backward)  2.22 us
  transfers between devices with their start and end apart: 12, of which 3 were waited for; matrix products, arithmetic and copies ran while one was open for 53% of the time, Pallas kernels for 0%

commit v1 on v0

v1 whole, which is shorter than its diff:
```python
import functools
import math

import jax
import jax.numpy as jnp
from jax import lax
from jax.experimental import pallas as pl
from jax.experimental.pallas import tpu as pltpu
from jax.sharding import PartitionSpec as P

NB = 2
R = 4
LANES = 128
STEP = 64
EPS = 0.0001 / (R * R)


def splits(value):
    high = value.astype(jnp.bfloat16).astype(jnp.float32)
    rest = value - high
    middle = rest.astype(jnp.bfloat16).astype(jnp.float32)
    return high, middle, rest - middle


def rounded_splits(value):
    high = lax.reduce_precision(value, 8, 7)
    rest = value - high
    middle = lax.reduce_precision(rest, 8, 7)
    return high, middle, rest - middle


def own_factors(own, weighted):
    scaled = (own[:, :3] - CENTRE.reshape(1, 3, 1)) * (1.0 / R)
    norm = jnp.sum(scaled * scaled, axis=1, keepdims=True)
    one = jnp.ones_like(norm)
    rows = jnp.concatenate(
        [-2.0 * scaled, one, norm, weighted[:, None], jnp.zeros_like(scaled[:, :2])], axis=1
    )
    high, middle, low = rounded_splits(rows)
    stacked = jnp.concatenate([high, high, middle, middle, high, low], axis=1)
    return jnp.swapaxes(stacked, 1, 2).astype(jnp.bfloat16)


def pairs_kernel(
    offsets, tile_count, info, counts, lists, left_ref, *refs, slots_of, with_back
):
    partner_refs = refs[: slots_of]
    rest = refs[slots_of :]
    if with_back:
        gained_ref, back_ref, acc_ref, wide_ref, right_ref = rest
        back_ref[...] = jnp.zeros_like(back_ref)
    else:
        gained_ref, acc_ref, right_ref = rest
    tile_len = left_ref.shape[1]
    width = left_ref.shape[2]
    sub = lax.broadcasted_iota(jnp.int32, (8, tile_len), 0)
    ones = jnp.ones((8, LANES), jnp.float32)
    pick = (lax.broadcasted_iota(jnp.int32, (width, LANES), 0) % 8 == 5) & (
        (lax.broadcasted_iota(jnp.int32, (width, LANES), 0) // 8 == 0)
        | (lax.broadcasted_iota(jnp.int32, (width, LANES), 0) // 8 == 2)
        | (lax.broadcasted_iota(jnp.int32, (width, LANES), 0) // 8 == 5)
    )
    pick = pick.astype(jnp.float32).astype(jnp.bfloat16)

    def one_tile(t, carry):
        acc_ref[...] = jnp.zeros_like(acc_ref)
        count = counts[t]
        if with_back:
            wide_ref[...] = jnp.dot(left_ref[t], pick, preferred_element_type=jnp.float32)
        for at, (offset, buffer) in enumerate(offsets):
            for n in range(NB):
                p = lists[at, t * NB + n]
                slab = p // tile_count
                tile = p - slab * tile_count
                valid = info[slab]
                slot = info[3 + slab]
                base = info[6 + at]

                @pl.when(valid > 0)
                def _(at=at, offset=offset, buffer=buffer, slab=slab, tile=tile, slot=slot, base=base):
                    theirs = partner_refs[buffer][base, slot, tile]
                    lift = (slab - 1).astype(jnp.float32) * (2.0 * R)
                    move = [offset - 0.5, lift - R, -float(R)]
                    coord = [
                        (theirs[i : i + 1] + move[i]) * (1.0 / R) for i in range(3)
                    ]
                    norm = coord[0] * coord[0] + coord[1] * coord[1] + coord[2] * coord[2] + EPS
                    zero = jnp.zeros((8, tile_len), jnp.float32)
                    rows = jnp.where(sub == 0, coord[0], zero)
                    rows = jnp.where(sub == 1, coord[1], rows)
                    rows = jnp.where(sub == 2, coord[2], rows)
                    rows = jnp.where(sub == 3, norm, rows)
                    rows = jnp.where(sub == 4, 1.0, rows)
                    high, middle, low = splits(rows)
                    right_ref[...] = jnp.concatenate(
                        [high, middle, high, middle, low, high], axis=0
                    ).astype(jnp.bfloat16)
                    their_weight = jnp.broadcast_to(theirs[3:4], (8, tile_len))
                    row = slot * tile_count + tile

                    def chunk(i, handed):
                        start = pl.multiple_of(i * STEP, STEP)
                        squared = jnp.dot(
                            left_ref[t, pl.ds(start, STEP), :],
                            right_ref[...],
                            preferred_element_type=jnp.float32,
                        )
                        for j in range(STEP // 8):
                            d2 = jnp.maximum(squared[j * 8 : j * 8 + 8], EPS)
                            q = d2 * lax.rsqrt(d2)
                            u = jnp.maximum(2.0 - q, 0.0)
                            v = jnp.maximum(u - 1.0, 0.0)
                            w = (u * u) * (0.25 * u) - (v * v) * v
                            g = w * their_weight
                            total = g[:, :LANES]
                            for h in range(1, tile_len // LANES):
                                total = total + g[:, h * LANES : (h + 1) * LANES]
                            rows_at = pl.ds(start + j * 8, 8)
                            acc_ref[rows_at, :] = acc_ref[rows_at, :] + total
                            if with_back:
                                mine = wide_ref[rows_at, :]
                                mine = jnp.concatenate([mine] * (tile_len // LANES), axis=1)
                                handed = handed + w * mine
                        return handed

                    handed = lax.fori_loop(
                        0, (count + (STEP - 1)) // STEP, chunk, jnp.zeros((8, tile_len), jnp.float32)
                    )
                    if with_back:
                        back_ref[at, pl.ds(row, 1), :] = back_ref[at, pl.ds(row, 1), :] + jnp.sum(
                            handed, axis=0, keepdims=True
                        )

        sums = lax.dot_general(
            ones,
            acc_ref[...],
            (((1,), (1,)), ((), ())),
            precision=lax.Precision.HIGHEST,
            preferred_element_type=jnp.float32,
        )
        gained_ref[pl.ds(t, 1), :] = sums[0:1]
        return carry

    lax.fori_loop(0, tile_count, one_tile, 0)


def pairs(info, counts, lists, left, buffers, offsets, with_back, name):
    tile_count, tile_len, width = left.shape
    slabs = buffers[0].shape[1]
    out_shape = [jax.ShapeDtypeStruct((tile_count, tile_len), jnp.float32)]
    scratch = [pltpu.VMEM((tile_len, LANES), jnp.float32)]
    if with_back:
        out_shape.append(
            jax.ShapeDtypeStruct((len(offsets), slabs * tile_count, tile_len), jnp.float32)
        )
        scratch.append(pltpu.VMEM((tile_len, LANES), jnp.float32))
    scratch.append(pltpu.VMEM((width, tile_len), jnp.bfloat16))
    smem = pl.BlockSpec(memory_space=pltpu.SMEM)
    vmem = pl.BlockSpec(memory_space=pltpu.VMEM)
    return pl.pallas_call(
        functools.partial(
            pairs_kernel,
            offsets,
            tile_count,
            slots_of=len(buffers),
            with_back=with_back,
        ),
        out_shape=out_shape,
        in_specs=[smem, smem, smem, vmem] + [vmem] * len(buffers),
        out_specs=[vmem] * len(out_shape),
        scratch_shapes=scratch,
        name=name,
    )(info, counts, lists, left, *buffers)


CENTRE = jnp.array([0.5, float(R), float(R)], jnp.float32)


def around(block, distance):
    size = lax.axis_size("chan")
    return lax.ppermute(block, "chan", [((i - distance) % size, i) for i in range(size)])


def exchange(block):
    size = lax.axis_size("chan")
    return lax.ppermute(block, "chan", [(i ^ 1, i) for i in range(size)])


def from_wall(block, distance):
    size = lax.axis_size("wall")
    route = [(i - distance, i) for i in range(size) if 0 <= i - distance < size]
    return lax.ppermute(block, "wall", route)


def on_device(coords, masses, counts, lists):
    tile_count = counts.shape[2]
    tile_len = masses.shape[2] // tile_count
    walls = lax.axis_size("wall")
    two = walls == 2
    wall = lax.axis_index("wall")
    odd = lax.axis_index("chan") % 2
    own_counts = counts[0, 0]
    slots = jnp.arange(tile_len, dtype=jnp.int32)
    filled = (slots[None, :] < own_counts[:, None]).astype(jnp.float32)
    weighted = masses.reshape(tile_count, tile_len) * filled
    own = jnp.concatenate(
        [jnp.swapaxes(coords.reshape(3, tile_count, tile_len), 0, 1), weighted[:, None]], axis=1
    )
    if two:
        swap = [(0, 1), (1, 0)]
        block = jnp.stack([own, lax.ppermute(own, "wall", swap)])
    else:
        block = jnp.stack([own, from_wall(own, 1), from_wall(own, -1)])
    near, far = around(block, -2), around(block, -4)
    left = own_factors(own, weighted)
    held = jnp.stack([block, near, far])
    other = exchange(held)

    low_ok = (wall > 0).astype(jnp.int32)
    high_ok = (wall < walls - 1).astype(jnp.int32)
    one = jnp.ones((), jnp.int32)
    head = [low_ok, one, high_ok, one, 0 * one, (1 if two else 2) * one]
    rows = lists[0, 0].reshape(R + 1, tile_count * NB)
    call = functools.partial(pairs, left=left)
    (gained_0,) = call(
        jnp.stack(head + [0 * one]), own_counts, rows[:1], buffers=[block[None]],
        offsets=((0.0, 0),), with_back=False, name="same",
    )
    gained_odd, back_odd = call(
        jnp.stack(head + [odd, odd + 1]), own_counts, rows[1:4:2], buffers=[other],
        offsets=((1.0, 0), (3.0, 0)), with_back=True, name="odd",
    )
    gained_even, back_even = call(
        jnp.stack(head + [1 * one, 2 * one]), own_counts, rows[2:5:2], buffers=[held],
        offsets=((2.0, 0), (4.0, 0)), with_back=True, name="even",
    )
    passed = exchange(back_odd)
    is_odd = odd > 0
    here = jnp.where(is_odd, passed[0], 0.0)
    to_near = back_even[0] + jnp.where(is_odd, passed[1], passed[0])
    to_far = back_even[1] + jnp.where(is_odd, 0.0, passed[1])
    returns = around(to_near, 2) + around(to_far, 4) + here
    returns = returns.reshape(-1, tile_count, tile_len)
    total = gained_0 + gained_odd + gained_even + returns[0]
    if two:
        total = total + lax.ppermute(returns[1], "wall", swap)
    else:
        total = total + from_wall(returns[2], 1) + from_wall(returns[1], -1)
    return (total * filled * (1.0 / (math.pi * NB * tile_len))).reshape(1, 1, -1)


def solution(mesh):
    placed = (
        P(None, "chan", "wall", None),
        P("chan", "wall", None),
        P("chan", "wall", None),
        P("chan", "wall", None, None, None),
    )
    return jax.shard_map(
        on_device, mesh=mesh, in_specs=placed, out_specs=P("chan", "wall", None), check_vma=False
    )
```

time: 104 us -> 121 us (1.16)
  Pallas kernels: 0 us -> 74.7 us
  other arithmetic: 61.6 us -> 3.01 us
  waiting for transfers between devices: 6.55 us -> 9.74 us
  starting transfers between devices: 23 us -> 21.6 us
  loops' own time: 1.3 us -> 0 us
    pallas_call x0 -> x3, Pallas kernels: none -> 74.7 us  [pairs(): pl.pallas_call(functools.partial(pairs_kernel, offsets, tile_count, slots...]
    reduce_sum x20 -> x1, other arithmetic: 56.2 us -> 0.12 us  [own_factors(): norm = jnp.sum(scaled * scaled, axis=1, keepdims=True)]
    unnamed x6 -> x23, local copies, waits for them, and re-layouts: 0.01 us -> 4.7 us
    ppermute x12 -> x8, waiting for transfers between devices: 6.55 us -> 9.74 us  [the longest x4 9.25 us: around(): lax.ppermute(block, 'chan', [((i - distance) % size, i) for i in range(si...]
    gather x5 -> x0, local copies, waits for them, and re-layouts: 3.16 us -> none  [pair_block(): jnp.take(partner, partner_rows.reshape(-1), axis=1)]
    add x21 -> x0, local copies, waits for them, and re-layouts: 1.87 us -> none  [the longest x20 1.86 us: single_tile(): theirs[1][:, None, :] + shift_y[:, None, None]]
    ppermute x12 -> x8, starting transfers between devices: 23 us -> 21.6 us  [the longest x4 16 us: around(): lax.ppermute(block, 'chan', [((i - distance) % size, i) for i in range(si...]
    another operation x18 -> x4, local copies, waits for them, and re-layouts: 0.6 us -> 1.93 us  [the longest x1 0.68 us: on_device(): jnp.stack(head + [1 * one, 2 * one])]
  transfers between devices with their start and end apart: 12 -> 8, of which waited for: 3 -> 5; matrix products, arithmetic and copies ran while one was open for 53% -> 5% of each run, Pallas kernels for 0% -> 38%
where the time goes in v1:
time: 121 us; the launch traced here: 120 us
  Pallas kernels  74.7 us (62%)
  starting transfers between devices  21.6 us (18%)
  local copies, waits for them, and re-layouts  10.3 us (9%)
  waiting for transfers between devices  9.74 us (8%)
  other arithmetic  3.01 us (2%)
    pallas_call x3, Pallas kernels, pairs(): pl.pallas_call(functools.partial(pairs_kernel, offsets, tile_count, slots...  74.7 us
    ppermute x4, starting transfers between devices, around(): lax.ppermute(block, 'chan', [((i - distance) % size, i) for i in range(si...  16 us
    ppermute x4, waiting for transfers between devices, around(): lax.ppermute(block, 'chan', [((i - distance) % size, i) for i in range(si...  9.25 us
    unnamed x23, local copies, waits for them, and re-layouts  4.7 us
    ppermute x1, starting transfers between devices, on_device(): block = jnp.stack([own, lax.ppermute(own, 'wall', swap)])  3.03 us
    ppermute x2, starting transfers between devices, exchange(): return lax.ppermute(block, 'chan', [(i ^ 1, i) for i in range(size)])  2.44 us
  transfers between devices with their start and end apart: 8, of which 5 were waited for; matrix products, arithmetic and copies ran while one was open for 5% of the time, Pallas kernels for 38%

profile of v1, /device:TPU:0, one launch (start us, length us, event | category | flops | bytes accessed | tf_op | source)
XLA Modules:
  0.0 119.5 jit_solution(4787959085216581024)
XLA Ops:
  0.0 0.0 copy-start.3
  0.0 0.9 reduce
  0.9 0.0 copy-start.6
  1.0 0.0 copy-done.3
  1.0 0.6 copy-done.6
  1.6 0.1 compare_select_fusion
  1.7 3.0 %collective-permute-start = (f32[16,4,256]{2,1,0:T(4,128)S(1)}, f32[16,4,256]{2,1,0:T(4,128)S(1)}, u32[]{:S(2)}, u32[]{:S(2)}) collective-permute-start(f32[16,4,256]{2,1,0:T(4,128)S(1)} %pad_maximum_fusion.2), channel_id=1, source_target_pairs={{0,1},{1,0},{2,3},{3,2},{4,5},{5,4},{6,7},{7,6},{8,9},{9,8},{10,11... | collective-permute-start | bytes 196616 | tf_op jit(solution)/shard_map/ppermute | solution.py:211
  4.8 0.0 copy-start.8
  4.8 0.7 copy-done.8
  5.5 0.0 copy-start.9
  5.5 0.1 copy.14
  5.5 0.6 copy-done.9
  6.1 0.1 multiply_reduce_fusion
  6.3 0.1 concatenate.10
  6.5 0.5 collective-permute-done
  7.1 0.0 copy-start.1
  7.1 4.2 %collective-permute-start.2 = (f32[2,16,4,256]{3,2,1,0:T(4,128)S(1)}, f32[2,16,4,256]{3,2,1,0:T(4,128)S(1)}, u32[]{:S(2)}, u32[]{:S(2)}) collective-permute-start(f32[2,16,4,256]{3,2,1,0:T(4,128)S(1)} %get-tuple-element.16), channel_id=1, source_target_pairs={{8,0},{10,2},{12,4},{14,6},{16,8},{18,10},{20,12},{22,14},{24,16},... | collective-permute-start | bytes 393224 | tf_op jit(solution)/shard_map/ppermute | solution.py:181
  11.2 1.4 %collective-permute-start.1 = (f32[2,16,4,256]{3,2,1,0:T(4,128)S(1)}, f32[2,16,4,256]{3,2,1,0:T(4,128)S(1)}, u32[]{:S(2)}, u32[]{:S(2)}) collective-permute-start(f32[2,16,4,256]{3,2,1,0:T(4,128)S(1)} %get-tuple-element.16), channel_id=1, source_target_pairs={{4,0},{6,2},{8,4},{10,6},{12,8},{14,10},{16,12},{18,14},{20,16},{2... | collective-permute-start | bytes 393224 | tf_op jit(solution)/shard_map/ppermute | solution.py:181
  12.7 1.6 %collective-permute-done.2 = f32[2,16,4,256]{3,2,1,0:T(4,128)S(1)} collective-permute-done((f32[2,16,4,256]{3,2,1,0:T(4,128)S(1)}, f32[2,16,4,256]{3,2,1,0:T(4,128)S(1)}, u32[]{:S(2)}, u32[]{:S(2)}) %collective-permute-start.2) | collective-permute-done | bytes 131104 | tf_op jit(solution)/shard_map/ppermute | solution.py:181
  14.3 2.0 %collective-permute-done.1 = f32[2,16,4,256]{3,2,1,0:T(4,128)S(1)} collective-permute-done((f32[2,16,4,256]{3,2,1,0:T(4,128)S(1)}, f32[2,16,4,256]{3,2,1,0:T(4,128)S(1)}, u32[]{:S(2)}, u32[]{:S(2)}) %collective-permute-start.1) | collective-permute-done | bytes 131104 | tf_op jit(solution)/shard_map/ppermute | solution.py:181
  16.2 0.1 pad_maximum_fusion.refs_0_
  16.3 0.0 copy-done.1
  16.3 0.0 copy-start
  16.3 0.1 collective-permute-start.3
  16.5 1.3 %copy.13.left_ref = bf16[16,256,48]{2,1,0:T(8,128)(2,1)} copy(bf16[16,256,48]{1,2,0:T(8,128)(2,1)S(1)} %bitcast.29) | data formatting | bytes 786432 | tf_op jit(solution)/shard_map/convert_element_type | solution.py:41
  17.8 0.0 copy-done
  17.8 0.1 slice.36
  17.9 0.6 copy.19.lists
  18.5 0.7 stack.60.info
  19.2 0.0 collective-permute-done.3.refs_0_
  19.2 0.0 copy-start.2
  19.2 0.7 copy-done.2
  19.9 28.7 %odd.1 = (f32[16,256]{1,0:T(8,128)}, f32[2,32,256]{2,1,0:T(8,128)}) custom-call(s32[8]{0:T(128)} %stack.60.info, s32[16]{0:T(128)} %bitcast.36, s32[2,32]{1,0:T(2,128)} %copy.19.lists, bf16[16,256,48]{2,1,0:T(8,128)(2,1)} %copy.13.left_ref, f32[3,2,16,4,256]{4,3,2,1,0:T(4,128)} %copy-done.2), custom_call_target="tpu_custom_call" | custom-call | tf_op jit(solution)/shard_map/odd/pallas_call | solution.py:160
  48.6 2.4 %collective-permute-start.4 = (f32[2,32,256]{2,1,0:T(8,128)}, f32[2,32,256]{2,1,0:T(8,128)S(1)}, u32[]{:S(2)}, u32[]{:S(2)}) collective-permute-start(f32[2,32,256]{2,1,0:T(8,128)} %get-tuple-element.12), channel_id=1, source_target_pairs={{2,0},{0,2},{6,4},{4,6},{10,8},{8,10},{14,12},{12,14},{18,16},{16,... | collective-permute-start | bytes 196616 | tf_op jit(solution)/shard_map/ppermute | solution.py:186
  51.0 0.1 slice.37
  51.1 0.7 copy.20.lists
  51.8 0.7 stack.64.info
  52.4 29.3 %even.1 = (f32[16,256]{1,0:T(8,128)}, f32[2,32,256]{2,1,0:T(8,128)}) custom-call(s32[8]{0:T(128)} %stack.64.info, s32[16]{0:T(128)} %bitcast.37, s32[2,32]{1,0:T(2,128)} %copy.20.lists, bf16[16,256,48]{2,1,0:T(8,128)(2,1)} %copy.13.left_ref, f32[3,2,16,4,256]{4,3,2,1,0:T(4,128)} %copy-done), custom_call_target="tpu_custom_call" | custom-call | tf_op jit(solution)/shard_map/even/pallas_call | solution.py:160
  81.7 0.0 collective-permute-done.4
  81.7 0.8 add_bitcast_fusion
  82.5 10.4 %collective-permute-start.5 = (f32[32,256]{1,0:T(8,128)S(1)}, f32[32,256]{1,0:T(8,128)S(1)}, u32[]{:S(2)}, u32[]{:S(2)}) collective-permute-start(f32[32,256]{1,0:T(8,128)S(1)} %get-tuple-element.14), channel_id=1, source_target_pairs={{28,0},{30,2},{0,4},{2,6},{4,8},{6,10},{8,12},{10,14},{12,16},{14,... | collective-permute-start | bytes 98312 | tf_op jit(solution)/shard_map/ppermute | solution.py:181
  92.9 0.0 collective-permute-start.6
  93.0 1.6 %collective-permute-done.5 = f32[32,256]{1,0:T(8,128)S(1)} collective-permute-done((f32[32,256]{1,0:T(8,128)S(1)}, f32[32,256]{1,0:T(8,128)S(1)}, u32[]{:S(2)}, u32[]{:S(2)}) %collective-permute-start.5) | collective-permute-done | bytes 32800 | tf_op jit(solution)/shard_map/ppermute | solution.py:181
  94.5 4.1 %collective-permute-done.6 = f32[32,256]{1,0:T(8,128)S(1)} collective-permute-done((f32[32,256]{1,0:T(8,128)S(1)}, f32[32,256]{1,0:T(8,128)S(1)}, u32[]{:S(2)}, u32[]{:S(2)}) %collective-permute-start.6) | collective-permute-done | bytes 32800 | tf_op jit(solution)/shard_map/ppermute | solution.py:181
  98.7 0.1 collective-permute-start.7
  98.8 0.6 stack.54.info
  99.3 0.0 slice-start
  99.3 0.7 slice-done
  100.0 0.1 copy.11
  100.1 0.6 slice.35.lists
  100.7 0.0 copy-start.4
  100.7 0.0 copy-start.5
  100.7 16.7 %same.1 = f32[16,256]{1,0:T(8,128)} custom-call(s32[7]{0:T(128)} %stack.54.info, s32[16]{0:T(128)} %bitcast.38, s32[1,32]{1,0:T(1,128)} %slice.35.lists, bf16[16,256,48]{2,1,0:T(8,128)(2,1)} %copy.13.left_ref, f32[1,2,16,4,256]{4,3,2,1,0:T(4,128)} %copy-done.1), custom_call_target="tpu_custom_call" | custom-call | tf_op jit(solution)/shard_map/same/pallas_call | solution.py:160
  117.5 0.0 collective-permute-done.7
  117.5 0.0 copy-start.7
  117.5 0.0 copy-done.4
  117.5 0.0 copy-done.5
  117.5 0.6 copy-done.7
  118.1 0.8 fusion.4
  118.9 0.6 reshape.77
  (15 shorter events, 0.2 us)
Async XLA Ops:
  0.0 1.0 copy-start.3
  0.9 0.7 copy-start.6
  1.7 5.3 %collective-permute-start = (f32[16,4,256]{2,1,0:T(4,128)S(1)}, f32[16,4,256]{2,1,0:T(4,128)S(1)}, u32[]{:S(2)}, u32[]{:S(2)}) collective-permute-start(f32[16,4,256]{2,1,0:T(4,128)S(1)} %pad_maximum_fusion.2), channel_id=1, source_target_pairs={{0,1},{1,0},{2,3},{3,2},{4,5},{5,4},{6,7},{7,6},{8,9},{9,8},{10,11... | collective-permute-start | bytes 196616 | tf_op jit(solution)/shard_map/ppermute | solution.py:211
  4.8 0.7 copy-start.8
  5.5 0.7 copy-start.9
  7.1 9.3 %copy-start.1 = (f32[1,2,16,4,256]{4,3,2,1,0:T(4,128)}, f32[1,2,16,4,256]{4,3,2,1,0:T(4,128)S(1)}, u32[]{:S(2)}) copy-start(f32[1,2,16,4,256]{4,3,2,1,0:T(4,128)S(1)} %get-tuple-element.15.refs_0_) | copy-start | bytes 393220
  7.1 7.2 %collective-permute-start.2 = (f32[2,16,4,256]{3,2,1,0:T(4,128)S(1)}, f32[2,16,4,256]{3,2,1,0:T(4,128)S(1)}, u32[]{:S(2)}, u32[]{:S(2)}) collective-permute-start(f32[2,16,4,256]{3,2,1,0:T(4,128)S(1)} %get-tuple-element.16), channel_id=1, source_target_pairs={{8,0},{10,2},{12,4},{14,6},{16,8},{18,10},{20,12},{22,14},{24,16},... | collective-permute-start | bytes 393224 | tf_op jit(solution)/shard_map/ppermute | solution.py:181
  11.2 5.0 %collective-permute-start.1 = (f32[2,16,4,256]{3,2,1,0:T(4,128)S(1)}, f32[2,16,4,256]{3,2,1,0:T(4,128)S(1)}, u32[]{:S(2)}, u32[]{:S(2)}) collective-permute-start(f32[2,16,4,256]{3,2,1,0:T(4,128)S(1)} %get-tuple-element.16), channel_id=1, source_target_pairs={{4,0},{6,2},{8,4},{10,6},{12,8},{14,10},{16,12},{18,14},{20,16},{2... | collective-permute-start | bytes 393224 | tf_op jit(solution)/shard_map/ppermute | solution.py:181
  16.3 1.5 %copy-start = (f32[3,2,16,4,256]{4,3,2,1,0:T(4,128)}, f32[3,2,16,4,256]{4,3,2,1,0:T(4,128)S(1)}, u32[]{:S(2)}) copy-start(f32[3,2,16,4,256]{4,3,2,1,0:T(4,128)S(1)} %pad_maximum_fusion.refs_0_) | copy-start | bytes 1179652
  16.3 2.9 %collective-permute-start.3 = (f32[3,2,16,4,256]{4,3,2,1,0:T(4,128)S(1)}, f32[3,2,16,4,256]{4,3,2,1,0:T(4,128)S(1)}, u32[]{:S(2)}, u32[]{:S(2)}) collective-permute-start(f32[3,2,16,4,256]{4,3,2,1,0:T(4,128)S(1)} %pad_maximum_fusion.refs_0_), channel_id=1, source_target_pairs={{2,0},{0,2},{6,4},{4,6},{10,8},{8,10},{14,12},{12,14},{18,16},{16,... | collective-permute-start | bytes 1179656 | tf_op jit(solution)/shard_map/ppermute | solution.py:186
  19.2 0.7 copy-start.2
  48.6 33.1 %collective-permute-start.4 = (f32[2,32,256]{2,1,0:T(8,128)}, f32[2,32,256]{2,1,0:T(8,128)S(1)}, u32[]{:S(2)}, u32[]{:S(2)}) collective-permute-start(f32[2,32,256]{2,1,0:T(8,128)} %get-tuple-element.12), channel_id=1, source_target_pairs={{2,0},{0,2},{6,4},{4,6},{10,8},{8,10},{14,12},{12,14},{18,16},{16,... | collective-permute-start | bytes 196616 | tf_op jit(solution)/shard_map/ppermute | solution.py:186
  82.5 12.0 %collective-permute-start.5 = (f32[32,256]{1,0:T(8,128)S(1)}, f32[32,256]{1,0:T(8,128)S(1)}, u32[]{:S(2)}, u32[]{:S(2)}) collective-permute-start(f32[32,256]{1,0:T(8,128)S(1)} %get-tuple-element.14), channel_id=1, source_target_pairs={{28,0},{30,2},{0,4},{2,6},{4,8},{6,10},{8,12},{10,14},{12,16},{14,... | collective-permute-start | bytes 98312 | tf_op jit(solution)/shard_map/ppermute | solution.py:181
  92.9 5.7 %collective-permute-start.6 = (f32[32,256]{1,0:T(8,128)S(1)}, f32[32,256]{1,0:T(8,128)S(1)}, u32[]{:S(2)}, u32[]{:S(2)}) collective-permute-start(f32[32,256]{1,0:T(8,128)S(1)} %get-tuple-element.13), channel_id=1, source_target_pairs={{24,0},{26,2},{28,4},{30,6},{0,8},{2,10},{4,12},{6,14},{8,16},{10,... | collective-permute-start | bytes 98312 | tf_op jit(solution)/shard_map/ppermute | solution.py:181
  98.7 18.8 %collective-permute-start.7 = (f32[16,256]{1,0:T(8,128)S(1)}, f32[16,256]{1,0:T(8,128)S(1)}, u32[]{:S(2)}, u32[]{:S(2)}) collective-permute-start(f32[16,256]{1,0:T(8,128)S(1)} %slice.47), channel_id=1, source_target_pairs={{0,1},{1,0},{2,3},{3,2},{4,5},{5,4},{6,7},{7,6},{8,9},{9,8},{10,11... | collective-permute-start | bytes 49160 | tf_op jit(solution)/shard_map/ppermute | solution.py:246
  99.3 0.7 slice-start
  100.7 16.7 %copy-start.4 = (f32[16,256]{1,0:T(8,128)S(1)}, f32[16,256]{1,0:T(8,128)}, u32[]{:S(2)}) copy-start(f32[16,256]{1,0:T(8,128)} %get-tuple-element.9) | copy-start | bytes 49156
  100.7 16.7 %copy-start.5 = (f32[16,256]{1,0:T(8,128)S(1)}, f32[16,256]{1,0:T(8,128)}, u32[]{:S(2)}) copy-start(f32[16,256]{1,0:T(8,128)} %get-tuple-element.10) | copy-start | bytes 49156
  117.5 0.7 copy-start.7

commit v2 on v1

v2 whole, which is shorter than its diff:
```python
import functools
import math

import jax
import jax.numpy as jnp
from jax import lax
from jax.experimental import pallas as pl
from jax.experimental.pallas import tpu as pltpu
from jax.sharding import PartitionSpec as P

NB = 2
R = 4
LANES = 128
STEP = 64
BATCH = 4
EPS = 0.0001 / (R * R)


def splits(value):
    high = value.astype(jnp.bfloat16).astype(jnp.float32)
    rest = value - high
    middle = rest.astype(jnp.bfloat16).astype(jnp.float32)
    return high, middle, rest - middle


def rounded_splits(value):
    high = lax.reduce_precision(value, 8, 7)
    rest = value - high
    middle = lax.reduce_precision(rest, 8, 7)
    return high, middle, rest - middle


def own_factors(own, weighted):
    scaled = (own[:, :3] - CENTRE.reshape(1, 3, 1)) * (1.0 / R)
    norm = jnp.sum(scaled * scaled, axis=1, keepdims=True)
    one = jnp.ones_like(norm)
    rows = jnp.concatenate(
        [-2.0 * scaled, one, norm, weighted[:, None], jnp.zeros_like(scaled[:, :2])], axis=1
    )
    high, middle, low = rounded_splits(rows)
    stacked = jnp.concatenate([high, high, middle, middle, high, low], axis=1)
    return jnp.swapaxes(stacked, 1, 2).astype(jnp.bfloat16)


def plan_kernel(groups, tile_count, per_tile, info, counts, lists, totals_ref, *plans):
    for group, offsets in enumerate(groups):
        plan = plans[group]

        def one_list(i, at_row, group=group, plan=plan):
            position, at, row = at_row
            t = i // NB
            p = lists[row, i]
            slab = p // tile_count
            tile = p - slab * tile_count
            slot = info[3 + slab]
            code = ((at * 3 + slot) * tile_count + tile) * (tile_count + 1) + t
            code = code * per_tile
            for c in range(per_tile):
                plan[position + c] = code + c
            chunks = (counts[t] + (STEP - 1)) // STEP
            return position + info[slab] * chunks, at, row

        position = jnp.int32(0)
        for at, row in enumerate(offsets):
            position, _, _ = lax.fori_loop(
                0, tile_count * NB, one_list, (position, jnp.int32(at), jnp.int32(row))
            )
        for c in range(3 * BATCH):
            plan[position + c] = tile_count * per_tile
        totals_ref[group] = position


def pairs_kernel(
    offsets, tile_count, group, info, totals, plan, left_ref, *refs, buffer_count, with_back
):
    partner_refs = refs[:buffer_count]
    rest = refs[buffer_count:]
    if with_back:
        gained_ref, back_ref, acc_ref, right_ref, first_ref, second_ref, wide_ref, sum_ref = rest
    else:
        gained_ref, acc_ref, right_ref, first_ref, second_ref = rest
    tile_len = left_ref.shape[1]
    width = left_ref.shape[2]
    slabs = partner_refs[0].shape[1]
    per_tile = tile_len // STEP
    halves = tile_len // LANES
    sub = lax.broadcasted_iota(jnp.int32, (8, tile_len), 0)
    spare = slabs * tile_count * len(offsets)

    acc_ref[...] = jnp.zeros_like(acc_ref)
    if with_back:
        sum_ref[...] = jnp.zeros_like(sum_ref)
        line = lax.broadcasted_iota(jnp.int32, (width, LANES), 0)
        block = line // 8
        pick = (line % 8 == 5) & ((block == 0) | (block == 2) | (block == 5))
        pick = pick.astype(jnp.float32).astype(jnp.bfloat16)

        def widen(i, carry):
            for j in range(2):
                t = i * 2 + j
                wide_ref[t] = jnp.dot(left_ref[t], pick, preferred_element_type=jnp.float32)
            return carry

        lax.fori_loop(0, tile_count // 2, widen, 0)

    for at, (offset, buffer) in enumerate(offsets):
        for slot in range(slabs):
            lift = (info[6 + slot] - 1).astype(jnp.float32) * (2.0 * R)
            move = [offset - 0.5, lift - R, -float(R)]
            base = info[9 + at]

            def factors(i, carry, at=at, buffer=buffer, slot=slot, move=move, base=base):
                for j in range(4):
                    tile = i * 4 + j
                    theirs = partner_refs[buffer][base, slot, tile]
                    x, y, z = [(theirs[c : c + 1] + move[c]) * (1.0 / R) for c in range(3)]
                    norm = x * x + y * y + z * z + EPS
                    rows = jnp.where(sub == 0, x, jnp.where(sub == 1, y, jnp.where(sub == 2, z, norm)))
                    rows = jnp.where(sub == 4, 1.0, jnp.where(sub > 4, 0.0, rows))
                    high, middle, low = splits(rows)
                    right_ref[(at * slabs + slot) * tile_count + tile] = jnp.concatenate(
                        [high, middle, high, middle, low, high], axis=0
                    ).astype(jnp.bfloat16)
                return carry

            lax.fori_loop(0, tile_count // 4, factors, 0)

    def decode(i):
        code = plan[i]
        pair = code // per_tile
        c = code - pair * per_tile
        where = pair // (tile_count + 1)
        t = pair - where * (tile_count + 1)
        lane = where // tile_count
        tile = where - lane * tile_count
        at = lane // 3
        slot = lane - at * 3
        return at, slot, tile, t, c

    def squares(start, out_ref):
        for j in range(BATCH):
            at, slot, tile, t, c = decode(start + j)
            own_tile = jnp.minimum(t, tile_count - 1)
            out_ref[j] = jnp.dot(
                left_ref[own_tile, pl.ds(pl.multiple_of(c * STEP, STEP), STEP), :],
                right_ref[(at * slabs + slot) * tile_count + tile],
                preferred_element_type=jnp.float32,
            )

    def weigh(start, in_ref):
        for j in range(BATCH):
            at, slot, tile, t, c = decode(start + j)
            theirs = partner_refs[0][info[9 + at], slot, tile, 3:4, :]
            their_weight = jnp.broadcast_to(theirs, (8, tile_len))
            handed = jnp.zeros((8, tile_len), jnp.float32)
            first_row = pl.multiple_of(c * STEP, STEP)
            for r in range(STEP // 8):
                d2 = jnp.maximum(in_ref[j, r * 8 : r * 8 + 8], EPS)
                q = d2 * lax.rsqrt(d2)
                u = jnp.maximum(2.0 - q, 0.0)
                v = jnp.maximum(u - 1.0, 0.0)
                w = (u * u) * (0.25 * u) - (v * v) * v
                g = w * their_weight
                total = g[:, :LANES]
                for h in range(1, halves):
                    total = total + g[:, h * LANES : (h + 1) * LANES]
                rows_at = pl.ds(first_row + r * 8, 8)
                acc_ref[t, rows_at, :] = acc_ref[t, rows_at, :] + total
                if with_back:
                    mine = wide_ref[t, rows_at, :]
                    handed = handed + w * jnp.concatenate([mine] * halves, axis=1)
            if with_back:
                row = jnp.where(t < tile_count, (at * slabs + slot) * tile_count + tile, spare)
                sum_ref[row] = sum_ref[row] + handed

    squares(0, first_ref)

    def two_batches(i, carry):
        start = i * (2 * BATCH)
        squares(start + BATCH, second_ref)
        weigh(start, first_ref)
        squares(start + 2 * BATCH, first_ref)
        weigh(start + BATCH, second_ref)
        return carry

    lax.fori_loop(0, (totals[group] + (2 * BATCH - 1)) // (2 * BATCH), two_batches, 0)

    ones = jnp.ones((8, LANES), jnp.bfloat16)

    def finish(i, carry):
        for j in range(4):
            t = i * 4 + j
            sums = jnp.zeros((8, tile_len), jnp.float32)
            for piece in splits(acc_ref[t]):
                sums = sums + lax.dot_general(
                    ones, piece.astype(jnp.bfloat16), (((1,), (1,)), ((), ())),
                    preferred_element_type=jnp.float32,
                )
            gained_ref[pl.ds(t, 1), :] = sums[0:1]
        return carry

    lax.fori_loop(0, tile_count // 4, finish, 0)
    if with_back:

        def fold(i, carry):
            for j in range(8):
                k = i * 8 + j
                back_ref[pl.ds(k, 1), :] = jnp.sum(sum_ref[k], axis=0, keepdims=True)
            return carry

        lax.fori_loop(0, spare // 8, fold, 0)


def pairs(info, totals, plan, left, buffers, offsets, with_back, group, name):
    tile_count, tile_len, width = left.shape
    slabs = buffers[0].shape[1]
    rows = len(offsets) * slabs * tile_count
    squares = pltpu.VMEM((BATCH, STEP, tile_len), jnp.float32)
    out_shape = [jax.ShapeDtypeStruct((tile_count, tile_len), jnp.float32)]
    scratch = [
        pltpu.VMEM((tile_count + 1, tile_len, LANES), jnp.float32),
        pltpu.VMEM((rows, width, tile_len), jnp.bfloat16),
        squares,
        squares,
    ]
    if with_back:
        out_shape.append(jax.ShapeDtypeStruct((rows, tile_len), jnp.float32))
        scratch.append(pltpu.VMEM((tile_count + 1, tile_len, LANES), jnp.float32))
        scratch.append(pltpu.VMEM((rows + 1, 8, tile_len), jnp.float32))
    smem = pl.BlockSpec(memory_space=pltpu.SMEM)
    vmem = pl.BlockSpec(memory_space=pltpu.VMEM)
    return pl.pallas_call(
        functools.partial(
            pairs_kernel, offsets, tile_count, group,
            buffer_count=len(buffers), with_back=with_back,
        ),
        out_shape=out_shape,
        in_specs=[smem, smem, smem, vmem] + [vmem] * len(buffers),
        out_specs=[vmem] * len(out_shape),
        scratch_shapes=scratch,
        name=name,
    )(info, totals, plan, left, *buffers)


def plans_of(info, counts, rows, groups, tile_len):
    tile_count = counts.shape[0]
    per_tile = tile_len // STEP
    smem = pl.BlockSpec(memory_space=pltpu.SMEM)
    lengths = [len(g) * tile_count * NB * per_tile + 4 * BATCH for g in groups]
    return pl.pallas_call(
        functools.partial(plan_kernel, groups, tile_count, per_tile),
        out_shape=[jax.ShapeDtypeStruct((len(groups),), jnp.int32)]
        + [jax.ShapeDtypeStruct((n,), jnp.int32) for n in lengths],
        in_specs=[smem] * 3,
        out_specs=[smem] * (1 + len(groups)),
        name="plan",
    )(info, counts, rows)


CENTRE = jnp.array([0.5, float(R), float(R)], jnp.float32)


def around(block, distance):
    size = lax.axis_size("chan")
    return lax.ppermute(block, "chan", [((i - distance) % size, i) for i in range(size)])


def exchange(block):
    size = lax.axis_size("chan")
    return lax.ppermute(block, "chan", [(i ^ 1, i) for i in range(size)])


def from_wall(block, distance):
    size = lax.axis_size("wall")
    route = [(i - distance, i) for i in range(size) if 0 <= i - distance < size]
    return lax.ppermute(block, "wall", route)


def on_device(coords, masses, counts, lists):
    tile_count = counts.shape[2]
    tile_len = masses.shape[2] // tile_count
    walls = lax.axis_size("wall")
    two = walls == 2
    wall = lax.axis_index("wall")
    odd = lax.axis_index("chan") % 2
    own_counts = counts[0, 0]
    slots = jnp.arange(tile_len, dtype=jnp.int32)
    filled = (slots[None, :] < own_counts[:, None]).astype(jnp.float32)
    weighted = masses.reshape(tile_count, tile_len) * filled
    own = jnp.concatenate(
        [jnp.swapaxes(coords.reshape(3, tile_count, tile_len), 0, 1), weighted[:, None]], axis=1
    )
    if two:
        swap = [(0, 1), (1, 0)]
        block = jnp.stack([own, lax.ppermute(own, "wall", swap)])
    else:
        block = jnp.stack([own, from_wall(own, 1), from_wall(own, -1)])
    near, far = around(block, -2), around(block, -4)
    left = own_factors(own, weighted)
    held = jnp.stack([block, near, far])
    other = exchange(held)

    low_ok = (wall > 0).astype(jnp.int32)
    high_ok = (wall < walls - 1).astype(jnp.int32)
    one = jnp.ones((), jnp.int32)
    walled = (wall > 0).astype(jnp.int32)
    if two:
        head = [low_ok, one, high_ok, one, 0 * one, one, one, 2 - 2 * walled, 0 * one]
    else:
        head = [low_ok, one, high_ok, one, 0 * one, 2 * one, one, 0 * one, 2 * one]
    near_at = 3 + odd
    info = jnp.stack(head + [near_at, one, near_at + 1, 2 * one])
    rows = lists[0, 0].reshape(R + 1, tile_count * NB)
    totals, plan_same, plan_ahead = plans_of(
        info, own_counts, rows, ((0,), (1, 2, 3, 4)), tile_len
    )
    (gained_same,) = pairs(
        jnp.stack(head + [0 * one]), totals, plan_same, left, [block[None]],
        ((0.0, 0),), False, 0, "same",
    )
    gained_ahead, back = pairs(
        info, totals, plan_ahead, left, [jnp.concatenate([held, other])],
        ((1.0, 0), (2.0, 0), (3.0, 0), (4.0, 0)), True, 1, "ahead",
    )
    back = back.reshape(R, -1, tile_len)
    back_odd, back_even = back[0::2], back[1::2]
    passed = exchange(back_odd)
    is_odd = odd > 0
    here = jnp.where(is_odd, passed[0], 0.0)
    to_near = back_even[0] + jnp.where(is_odd, passed[1], passed[0])
    to_far = back_even[1] + jnp.where(is_odd, 0.0, passed[1])
    returns = around(to_near, 2) + around(to_far, 4) + here
    returns = returns.reshape(-1, tile_count, tile_len)
    total = gained_same + gained_ahead + returns[0]
    if two:
        total = total + lax.ppermute(returns[1], "wall", swap)
    else:
        total = total + from_wall(returns[2], 1) + from_wall(returns[1], -1)
    return (total * filled * (1.0 / (math.pi * NB * tile_len))).reshape(1, 1, -1)


def solution(mesh):
    placed = (
        P(None, "chan", "wall", None),
        P("chan", "wall", None),
        P("chan", "wall", None),
        P("chan", "wall", None, None, None),
    )
    return jax.shard_map(
        on_device, mesh=mesh, in_specs=placed, out_specs=P("chan", "wall", None), check_vma=False
    )
```

time: 121 us -> 73 us (0.60)
  Pallas kernels: 74.7 us -> 37.3 us
  starting transfers between devices: 21.6 us -> 10.5 us
  waiting for transfers between devices: 9.74 us -> 13.3 us
  local copies, waits for them, and re-layouts: 10.3 us -> 7.04 us
    pallas_call x3, Pallas kernels: 74.7 us -> 37.3 us  [the longest x2 31.9 us: pairs(): pl.pallas_call(functools.partial(pairs_kernel, offsets, tile_count, group...]
    ppermute x4, starting transfers between devices: 16 us -> 7.11 us  [around(): lax.ppermute(block, 'chan', [((i - distance) % size, i) for i in range(si...]
    unnamed x23 -> x13, local copies, waits for them, and re-layouts: 4.7 us -> 2.1 us
    ppermute x4, waiting for transfers between devices: 9.25 us -> 11.7 us  [around(): lax.ppermute(block, 'chan', [((i - distance) % size, i) for i in range(si...]
    ppermute x2, starting transfers between devices: 2.44 us -> 0.14 us  [exchange(): return lax.ppermute(block, 'chan', [(i ^ 1, i) for i in range(size)])]
    ppermute x2, waiting for transfers between devices: 0.01 us -> 1.24 us  [exchange(): return lax.ppermute(block, 'chan', [(i ^ 1, i) for i in range(size)])]
  transfers between devices with their start and end apart: 8 -> 8, of which waited for: 5 -> 5; matrix products, arithmetic and copies ran while one was open for 5% -> 5% of each run, Pallas kernels for 38% -> 19%
where the time goes in v2:
time: 73 us; the launch traced here: 72.4 us
  Pallas kernels  37.3 us (51%)
  waiting for transfers between devices  13.3 us (18%)
  starting transfers between devices  10.5 us (14%)
  local copies, waits for them, and re-layouts  7.04 us (10%)
  other arithmetic  4.09 us (6%)
    pallas_call x2, Pallas kernels, pairs(): pl.pallas_call(functools.partial(pairs_kernel, offsets, tile_count, group...  31.9 us
    ppermute x4, waiting for transfers between devices, around(): lax.ppermute(block, 'chan', [((i - distance) % size, i) for i in range(si...  11.7 us
    ppermute x4, starting transfers between devices, around(): lax.ppermute(block, 'chan', [((i - distance) % size, i) for i in range(si...  7.11 us
    pallas_call x1, Pallas kernels, plans_of(): pl.pallas_call(functools.partial(plan_kernel, groups, tile_count, per_til...  5.33 us
    ppermute x1, starting transfers between devices, on_device(): block = jnp.stack([own, lax.ppermute(own, 'wall', swap)])  3.03 us
    unnamed x13, local copies, waits for them, and re-layouts  2.1 us
  transfers between devices with their start and end apart: 8, of which 5 were waited for; matrix products, arithmetic and copies ran while one was open for 5% of the time, Pallas kernels for 19%

profile of v2, /device:TPU:0, one launch (start us, length us, event | category | flops | bytes accessed | tf_op | source)
XLA Modules:
  0.0 72.4 jit_solution(1295556455790297904)
XLA Ops:
  0.0 0.0 copy-start.3
  0.0 0.7 copy-done.3
  0.7 0.8 %compare_select_fusion = f32[16,1,256]{2,1,0:T(1,128)S(1)} fusion(f32[16,1,256]{2,1,0:T(1,128)} %bitcast.37, s32[16]{0:T(128)S(1)} %bitcast.39), kind=kLoop, calls=%fused_computation.11 | loop fusion | flops 8192 | bytes 32832 | tf_op jit(solution)/shard_map/mul | solution.py:289
  1.5 0.9 %reduce = f32[3,4096]{1,0:T(4,128)S(1)} reduce(f32[3,1,1,4096]{3,2,1,0:T(1,128)} %param.5, f32[]{:T(128)} %constant.58), dimensions={1,2}, to_apply=%param.5.reduce_sub_computation | reduce | bytes 98308 | tf_op args[0]
  2.4 3.0 %collective-permute-start = (f32[16,4,256]{2,1,0:T(4,128)S(1)}, f32[16,4,256]{2,1,0:T(4,128)S(1)}, u32[]{:S(2)}, u32[]{:S(2)}) collective-permute-start(f32[16,4,256]{2,1,0:T(4,128)S(1)} %pad_maximum_fusion.3), channel_id=1, source_target_pairs={{0,1},{1,0},{2,3},{3,2},{4,5},{5,4},{6,7},{7,6},{8,9},{9,8},{10,11... | collective-permute-start | bytes 196616 | tf_op jit(solution)/shard_map/ppermute | solution.py:295
  5.5 0.0 copy-start.2
  5.5 0.7 copy-done.2
  6.2 0.1 copy.9
  6.3 0.0 copy-start.5
  6.3 0.7 copy.10.lists
  6.9 0.0 copy-done.5
  6.9 0.1 multiply_reduce_fusion
  7.1 0.1 concatenate.14
  7.3 0.4 collective-permute-done
  7.8 0.0 copy-start
  7.8 5.1 %collective-permute-start.1 = (f32[2,16,4,256]{3,2,1,0:T(4,128)S(1)}, f32[2,16,4,256]{3,2,1,0:T(4,128)S(1)}, u32[]{:S(2)}, u32[]{:S(2)}) collective-permute-start(f32[2,16,4,256]{3,2,1,0:T(4,128)S(1)} %get-tuple-element.20), channel_id=1, source_target_pairs={{4,0},{6,2},{8,4},{10,6},{12,8},{14,10},{16,12},{18,14},{20,16},{2... | collective-permute-start | bytes 393224 | tf_op jit(solution)/shard_map/ppermute | solution.py:265
  12.9 0.4 collective-permute-start.2
  13.4 2.5 %collective-permute-done.1 = f32[2,16,4,256]{3,2,1,0:T(4,128)S(1)} collective-permute-done((f32[2,16,4,256]{3,2,1,0:T(4,128)S(1)}, f32[2,16,4,256]{3,2,1,0:T(4,128)S(1)}, u32[]{:S(2)}, u32[]{:S(2)}) %collective-permute-start.1) | collective-permute-done | bytes 131104 | tf_op jit(solution)/shard_map/ppermute | solution.py:265
  15.9 2.0 %collective-permute-done.2 = f32[2,16,4,256]{3,2,1,0:T(4,128)S(1)} collective-permute-done((f32[2,16,4,256]{3,2,1,0:T(4,128)S(1)}, f32[2,16,4,256]{3,2,1,0:T(4,128)S(1)}, u32[]{:S(2)}, u32[]{:S(2)}) %collective-permute-start.2) | collective-permute-done | bytes 131104 | tf_op jit(solution)/shard_map/ppermute | solution.py:265
  17.9 0.1 pad_maximum_fusion.1
  18.0 0.1 collective-permute-start.3
  18.1 1.3 %copy.12.left_ref = bf16[16,256,48]{2,1,0:T(8,128)(2,1)} copy(bf16[16,256,48]{1,2,0:T(8,128)(2,1)S(1)} %bitcast.29) | data formatting | bytes 786432 | tf_op jit(solution)/shard_map/convert_element_type | solution.py:42
  19.4 0.6 stack.57.info
  20.0 5.3 %plan.1 = (s32[2]{0:T(128)}, s32[144]{0:T(256)}, s32[528]{0:T(1024)}) custom-call(s32[13]{0:T(128)} %stack.57.info, s32[16]{0:T(128)} %bitcast.38, s32[5,32]{1,0:T(8,128)} %copy.10.lists), custom_call_target="tpu_custom_call" | custom-call | tf_op jit(solution)/shard_map/plan/pallas_call | solution.py:250
  25.4 0.0 collective-permute-done.3
  25.4 0.0 copy-done
  25.4 1.1 %pad_maximum_fusion.refs_0_ = f32[6,2,16,4,256]{4,3,2,1,0:T(4,128)} fusion(f32[3,2,16,4,256]{4,3,2,1,0:T(4,128)S(1)} %collective-permute-done.3, f32[1,2,16,4,256]{4,3,2,1,0:T(4,128)S(1)} %bitcast.33, f32[1,2,16,4,256]{4,3,2,1,0:T(4,128)S(1)} %bitcast.31, f32[1,2,16,4,256]{4,3,2,1,0:T(4,128)S(1)} %get-tuple-element.19.refs_0_), kind=kLoop, calls=%fused_computation | loop fusion | flops 589824 | bytes 1572864 | tf_op jit(solution)/shard_map/concatenate | solution.py:322
  26.5 23.4 %ahead.1 = (f32[16,256]{1,0:T(8,128)}, f32[128,256]{1,0:T(8,128)}) custom-call(s32[13]{0:T(128)} %stack.57.info, s32[2]{0:T(128)} %get-tuple-element.10.totals, s32[528]{0:T(1024)} %get-tuple-element.12.plan, bf16[16,256,48]{2,1,0:T(8,128)(2,1)} %copy.12.left_ref, f32[6,2,16,4,256]{4,3,2,1,0:T(4,128)} %pad_maximum_fusion.refs_0_), custom_call_target="tpu_custom_call" | custom-call | tf_op jit(solution)/shard_map/ahead/pallas_call | solution.py:232
  50.0 0.9 %fusion.8 = (f32[2,32,256]{2,1,0:T(8,128)S(1)}, f32[2,32,256]{2,1,0:T(8,128)S(1)}) fusion(f32[4,32,256]{2,1,0:T(8,128)} %bitcast.34), kind=kLoop, calls=%fused_computation.29 | loop fusion | bytes 262144 | tf_op jit(solution)/shard_map/slice | solution.py:326
  50.8 0.1 collective-permute-start.4
  50.9 1.2 %collective-permute-done.4 = f32[2,32,256]{2,1,0:T(8,128)S(1)} collective-permute-done((f32[2,32,256]{2,1,0:T(8,128)S(1)}, f32[2,32,256]{2,1,0:T(8,128)S(1)}, u32[]{:S(2)}, u32[]{:S(2)}) %collective-permute-start.4) | collective-permute-done | bytes 65568 | tf_op jit(solution)/shard_map/ppermute | solution.py:270
  52.2 1.5 %collective-permute-start.6 = (f32[32,256]{1,0:T(8,128)S(1)}, f32[32,256]{1,0:T(8,128)S(1)}, u32[]{:S(2)}, u32[]{:S(2)}) collective-permute-start(f32[32,256]{1,0:T(8,128)S(1)} %get-tuple-element.15), channel_id=1, source_target_pairs={{24,0},{26,2},{28,4},{30,6},{0,8},{2,10},{4,12},{6,14},{8,16},{10,... | collective-permute-start | bytes 98312 | tf_op jit(solution)/shard_map/ppermute | solution.py:265
  53.7 0.0 collective-permute-start.5
  53.7 7.2 %collective-permute-done.6 = f32[32,256]{1,0:T(8,128)S(1)} collective-permute-done((f32[32,256]{1,0:T(8,128)S(1)}, f32[32,256]{1,0:T(8,128)S(1)}, u32[]{:S(2)}, u32[]{:S(2)}) %collective-permute-start.6) | collective-permute-done | bytes 32800 | tf_op jit(solution)/shard_map/ppermute | solution.py:265
  60.9 0.0 collective-permute-done.5
  60.9 0.2 collective-permute-start.7
  61.1 0.7 stack.54.info
  61.8 0.0 copy-start.1
  61.8 8.5 %same.1 = f32[16,256]{1,0:T(8,128)} custom-call(s32[10]{0:T(128)} %stack.54.info, s32[2]{0:T(128)} %get-tuple-element.10.totals, s32[144]{0:T(256)} %get-tuple-element.11.plan, bf16[16,256,48]{2,1,0:T(8,128)(2,1)} %copy.12.left_ref, f32[1,2,16,4,256]{4,3,2,1,0:T(4,128)} %copy-done), custom_call_target="tpu_custom_call" | custom-call | tf_op jit(solution)/shard_map/same/pallas_call | solution.py:232
  70.3 0.0 copy-start.4
  70.3 0.0 collective-permute-done.7
  70.3 0.0 copy-done.1
  70.3 0.6 copy-done.4
  71.0 0.8 %fusion.6 = f32[16,256]{1,0:T(8,128)S(1)} fusion(f32[16,256]{1,0:T(8,128)S(1)} %collective-permute-done.7, f32[32,256]{1,0:T(8,128)S(1)} %bitcast_add_fusion, f32[16,256]{1,0:T(8,128)} %same.1, f32[16,256]{1,0:T(8,128)S(1)} %copy-done.1, s32[16]{0:T(128)S(1)} %bitcast.40), kind=kLoop, calls=%fused_computation.21 | loop fusion | flops 24576 | bytes 81984 | tf_op jit(solution)/shard_map/mul | solution.py:339
  71.8 0.6 reshape.80
  (17 shorter events, 0.2 us)
Async XLA Ops:
  0.0 0.7 copy-start.3
  2.4 5.3 %collective-permute-start = (f32[16,4,256]{2,1,0:T(4,128)S(1)}, f32[16,4,256]{2,1,0:T(4,128)S(1)}, u32[]{:S(2)}, u32[]{:S(2)}) collective-permute-start(f32[16,4,256]{2,1,0:T(4,128)S(1)} %pad_maximum_fusion.3), channel_id=1, source_target_pairs={{0,1},{1,0},{2,3},{3,2},{4,5},{5,4},{6,7},{7,6},{8,9},{9,8},{10,11... | collective-permute-start | bytes 196616 | tf_op jit(solution)/shard_map/ppermute | solution.py:295
  5.5 0.7 copy-start.2
  6.3 0.7 copy-start.5
  7.8 17.6 %copy-start = (f32[1,2,16,4,256]{4,3,2,1,0:T(4,128)}, f32[1,2,16,4,256]{4,3,2,1,0:T(4,128)S(1)}, u32[]{:S(2)}) copy-start(f32[1,2,16,4,256]{4,3,2,1,0:T(4,128)S(1)} %get-tuple-element.19.refs_0_) | copy-start | bytes 393220
  7.8 8.2 %collective-permute-start.1 = (f32[2,16,4,256]{3,2,1,0:T(4,128)S(1)}, f32[2,16,4,256]{3,2,1,0:T(4,128)S(1)}, u32[]{:S(2)}, u32[]{:S(2)}) collective-permute-start(f32[2,16,4,256]{3,2,1,0:T(4,128)S(1)} %get-tuple-element.20), channel_id=1, source_target_pairs={{4,0},{6,2},{8,4},{10,6},{12,8},{14,10},{16,12},{18,14},{20,16},{2... | collective-permute-start | bytes 393224 | tf_op jit(solution)/shard_map/ppermute | solution.py:265
  12.9 5.0 %collective-permute-start.2 = (f32[2,16,4,256]{3,2,1,0:T(4,128)S(1)}, f32[2,16,4,256]{3,2,1,0:T(4,128)S(1)}, u32[]{:S(2)}, u32[]{:S(2)}) collective-permute-start(f32[2,16,4,256]{3,2,1,0:T(4,128)S(1)} %get-tuple-element.20), channel_id=1, source_target_pairs={{8,0},{10,2},{12,4},{14,6},{16,8},{18,10},{20,12},{22,14},{24,16},... | collective-permute-start | bytes 393224 | tf_op jit(solution)/shard_map/ppermute | solution.py:265
  18.0 7.4 %collective-permute-start.3 = (f32[3,2,16,4,256]{4,3,2,1,0:T(4,128)S(1)}, f32[3,2,16,4,256]{4,3,2,1,0:T(4,128)S(1)}, u32[]{:S(2)}, u32[]{:S(2)}) collective-permute-start(f32[3,2,16,4,256]{4,3,2,1,0:T(4,128)S(1)} %pad_maximum_fusion.1), channel_id=1, source_target_pairs={{2,0},{0,2},{6,4},{4,6},{10,8},{8,10},{14,12},{12,14},{18,16},{16,... | collective-permute-start | bytes 1179656 | tf_op jit(solution)/shard_map/ppermute | solution.py:270
  50.8 1.3 %collective-permute-start.4 = (f32[2,32,256]{2,1,0:T(8,128)S(1)}, f32[2,32,256]{2,1,0:T(8,128)S(1)}, u32[]{:S(2)}, u32[]{:S(2)}) collective-permute-start(f32[2,32,256]{2,1,0:T(8,128)S(1)} %get-tuple-element.17), channel_id=1, source_target_pairs={{2,0},{0,2},{6,4},{4,6},{10,8},{8,10},{14,12},{12,14},{18,16},{16,... | collective-permute-start | bytes 196616 | tf_op jit(solution)/shard_map/ppermute | solution.py:270
  52.2 8.7 %collective-permute-start.6 = (f32[32,256]{1,0:T(8,128)S(1)}, f32[32,256]{1,0:T(8,128)S(1)}, u32[]{:S(2)}, u32[]{:S(2)}) collective-permute-start(f32[32,256]{1,0:T(8,128)S(1)} %get-tuple-element.15), channel_id=1, source_target_pairs={{24,0},{26,2},{28,4},{30,6},{0,8},{2,10},{4,12},{6,14},{8,16},{10,... | collective-permute-start | bytes 98312 | tf_op jit(solution)/shard_map/ppermute | solution.py:265
  53.7 7.2 %collective-permute-start.5 = (f32[32,256]{1,0:T(8,128)S(1)}, f32[32,256]{1,0:T(8,128)S(1)}, u32[]{:S(2)}, u32[]{:S(2)}) collective-permute-start(f32[32,256]{1,0:T(8,128)S(1)} %get-tuple-element.16), channel_id=1, source_target_pairs={{28,0},{30,2},{0,4},{2,6},{4,8},{6,10},{8,12},{10,14},{12,16},{14,... | collective-permute-start | bytes 98312 | tf_op jit(solution)/shard_map/ppermute | solution.py:265
  60.9 9.4 %collective-permute-start.7 = (f32[16,256]{1,0:T(8,128)S(1)}, f32[16,256]{1,0:T(8,128)S(1)}, u32[]{:S(2)}, u32[]{:S(2)}) collective-permute-start(f32[16,256]{1,0:T(8,128)S(1)} %slice.41), channel_id=1, source_target_pairs={{0,1},{1,0},{2,3},{3,2},{4,5},{5,4},{6,7},{7,6},{8,9},{9,8},{10,11... | collective-permute-start | bytes 49160 | tf_op jit(solution)/shard_map/ppermute | solution.py:336
  61.8 8.5 %copy-start.1 = (f32[16,256]{1,0:T(8,128)S(1)}, f32[16,256]{1,0:T(8,128)}, u32[]{:S(2)}) copy-start(f32[16,256]{1,0:T(8,128)} %get-tuple-element.13) | copy-start | bytes 49156
  70.3 0.7 copy-start.4

commit v3 on v2

--- a/solution.py
+++ b/solution.py
@@ -42,22 +42,25 @@
     return jnp.swapaxes(stacked, 1, 2).astype(jnp.bfloat16)
 
 
-def plan_kernel(groups, tile_count, per_tile, info, counts, lists, totals_ref, *plans):
+def entry_stride(tile_count, per_tile):
+    return per_tile << tile_count.bit_length()
+
+
+def plan_kernel(groups, tile_count, per_tile, slabs, info, counts, lists, totals_ref, *plans):
     for group, offsets in enumerate(groups):
         plan = plans[group]
 
         def one_list(i, at_row, group=group, plan=plan):
             position, at, row = at_row
-            t = i // NB
+            t = lax.div(i, jnp.int32(NB))
             p = lists[row, i]
-            slab = p // tile_count
+            slab = lax.div(p, jnp.int32(tile_count))
             tile = p - slab * tile_count
-            slot = info[3 + slab]
-            code = ((at * 3 + slot) * tile_count + tile) * (tile_count + 1) + t
-            code = code * per_tile
+            right = (at * slabs + info[3 + slab]) * tile_count + tile
+            code = right * entry_stride(tile_count, per_tile) + t * per_tile
             for c in range(per_tile):
                 plan[position + c] = code + c
-            chunks = (counts[t] + (STEP - 1)) // STEP
+            chunks = lax.div(counts[t] + (STEP - 1), jnp.int32(STEP))
             return position + info[slab] * chunks, at, row
 
         position = jnp.int32(0)
@@ -76,11 +79,11 @@
     partner_refs = refs[:buffer_count]
     rest = refs[buffer_count:]
     if with_back:
-        gained_ref, back_ref, acc_ref, right_ref, first_ref, second_ref, wide_ref, sum_ref = rest
+        gained_ref, back_ref, acc_ref, right_ref, weight_ref, first_ref, second_ref, wide_ref, sum_ref = rest
     else:
-        gained_ref, acc_ref, right_ref, first_ref, second_ref = rest
-    tile_len = left_ref.shape[1]
-    width = left_ref.shape[2]
+        gained_ref, acc_ref, right_ref, weight_ref, first_ref, second_ref = rest
+    tile_len = partner_refs[0].shape[-1]
+    width = left_ref.shape[1]
     slabs = partner_refs[0].shape[1]
     per_tile = tile_len // STEP
     halves = tile_len // LANES
@@ -98,7 +101,8 @@
         def widen(i, carry):
             for j in range(2):
                 t = i * 2 + j
-                wide_ref[t] = jnp.dot(left_ref[t], pick, preferred_element_type=jnp.float32)
+                at = pl.ds(pl.multiple_of(t * tile_len, tile_len), tile_len)
+                wide_ref[at, :] = jnp.dot(left_ref[at, :], pick, preferred_element_type=jnp.float32)
             return carry
 
         lax.fori_loop(0, tile_count // 2, widen, 0)
@@ -107,7 +111,7 @@
         for slot in range(slabs):
             lift = (info[6 + slot] - 1).astype(jnp.float32) * (2.0 * R)
             move = [offset - 0.5, lift - R, -float(R)]
-            base = info[9 + at]
+            base = info[9 + at] if with_back else 0
 
             def factors(i, carry, at=at, buffer=buffer, slot=slot, move=move, base=base):
                 for j in range(4):
@@ -118,42 +122,39 @@
                     rows = jnp.where(sub == 0, x, jnp.where(sub == 1, y, jnp.where(sub == 2, z, norm)))
                     rows = jnp.where(sub == 4, 1.0, jnp.where(sub > 4, 0.0, rows))
                     high, middle, low = splits(rows)
-                    right_ref[(at * slabs + slot) * tile_count + tile] = jnp.concatenate(
+                    index = (at * slabs + slot) * tile_count + tile
+                    weight_ref[index] = jnp.broadcast_to(theirs[3:4], (8, tile_len))
+                    right_ref[index] = jnp.concatenate(
                         [high, middle, high, middle, low, high], axis=0
                     ).astype(jnp.bfloat16)
                 return carry
 
             lax.fori_loop(0, tile_count // 4, factors, 0)
 
+    stride = entry_stride(tile_count, per_tile)
+
     def decode(i):
         code = plan[i]
-        pair = code // per_tile
-        c = code - pair * per_tile
-        where = pair // (tile_count + 1)
-        t = pair - where * (tile_count + 1)
-        lane = where // tile_count
-        tile = where - lane * tile_count
-        at = lane // 3
-        slot = lane - at * 3
-        return at, slot, tile, t, c
+        right = lax.div(code, jnp.int32(stride))
+        chunk = code - right * stride
+        return right, chunk
 
     def squares(start, out_ref):
         for j in range(BATCH):
-            at, slot, tile, t, c = decode(start + j)
-            own_tile = jnp.minimum(t, tile_count - 1)
+            right, chunk = decode(start + j)
+            chunk = jnp.minimum(chunk, tile_count * per_tile - 1)
             out_ref[j] = jnp.dot(
-                left_ref[own_tile, pl.ds(pl.multiple_of(c * STEP, STEP), STEP), :],
-                right_ref[(at * slabs + slot) * tile_count + tile],
+                left_ref[pl.ds(pl.multiple_of(chunk * STEP, STEP), STEP), :],
+                right_ref[right],
                 preferred_element_type=jnp.float32,
             )
 
     def weigh(start, in_ref):
         for j in range(BATCH):
-            at, slot, tile, t, c = decode(start + j)
-            theirs = partner_refs[0][info[9 + at], slot, tile, 3:4, :]
-            their_weight = jnp.broadcast_to(theirs, (8, tile_len))
+            right, chunk = decode(start + j)
+            their_weight = weight_ref[right]
             handed = jnp.zeros((8, tile_len), jnp.float32)
-            first_row = pl.multiple_of(c * STEP, STEP)
+            first_row = pl.multiple_of(chunk * STEP, STEP)
             for r in range(STEP // 8):
                 d2 = jnp.maximum(in_ref[j, r * 8 : r * 8 + 8], EPS)
                 q = d2 * lax.rsqrt(d2)
@@ -165,12 +166,12 @@
                 for h in range(1, halves):
                     total = total + g[:, h * LANES : (h + 1) * LANES]
                 rows_at = pl.ds(first_row + r * 8, 8)
-                acc_ref[t, rows_at, :] = acc_ref[t, rows_at, :] + total
+                acc_ref[rows_at, :] = acc_ref[rows_at, :] + total
                 if with_back:
-                    mine = wide_ref[t, rows_at, :]
+                    mine = wide_ref[rows_at, :]
                     handed = handed + w * jnp.concatenate([mine] * halves, axis=1)
             if with_back:
-                row = jnp.where(t < tile_count, (at * slabs + slot) * tile_count + tile, spare)
+                row = jnp.where(chunk < tile_count * per_tile, right, spare)
                 sum_ref[row] = sum_ref[row] + handed
 
     squares(0, first_ref)
@@ -191,7 +192,7 @@
         for j in range(4):
             t = i * 4 + j
             sums = jnp.zeros((8, tile_len), jnp.float32)
-            for piece in splits(acc_ref[t]):
+            for piece in splits(acc_ref[pl.ds(pl.multiple_of(t * tile_len, tile_len), tile_len), :]):
                 sums = sums + lax.dot_general(
                     ones, piece.astype(jnp.bfloat16), (((1,), (1,)), ((), ())),
                     preferred_element_type=jnp.float32,
@@ -212,20 +213,21 @@
 
 
 def pairs(info, totals, plan, left, buffers, offsets, with_back, group, name):
-    tile_count, tile_len, width = left.shape
-    slabs = buffers[0].shape[1]
+    width = left.shape[1]
+    slabs, tile_count, _, tile_len = buffers[0].shape[1:]
     rows = len(offsets) * slabs * tile_count
     squares = pltpu.VMEM((BATCH, STEP, tile_len), jnp.float32)
     out_shape = [jax.ShapeDtypeStruct((tile_count, tile_len), jnp.float32)]
     scratch = [
-        pltpu.VMEM((tile_count + 1, tile_len, LANES), jnp.float32),
+        pltpu.VMEM(((tile_count + 1) * tile_len, LANES), jnp.float32),
         pltpu.VMEM((rows, width, tile_len), jnp.bfloat16),
+        pltpu.VMEM((rows, 8, tile_len), jnp.float32),
         squares,
         squares,
     ]
     if with_back:
         out_shape.append(jax.ShapeDtypeStruct((rows, tile_len), jnp.float32))
-        scratch.append(pltpu.VMEM((tile_count + 1, tile_len, LANES), jnp.float32))
+        scratch.append(pltpu.VMEM(((tile_count + 1) * tile_len, LANES), jnp.float32))
         scratch.append(pltpu.VMEM((rows + 1, 8, tile_len), jnp.float32))
     smem = pl.BlockSpec(memory_space=pltpu.SMEM)
     vmem = pl.BlockSpec(memory_space=pltpu.VMEM)
@@ -242,17 +244,18 @@
     )(info, totals, plan, left, *buffers)
 
 
-def plans_of(info, counts, rows, groups, tile_len):
+def plans_of(info, counts, rows, groups, tile_len, slabs):
     tile_count = counts.shape[0]
     per_tile = tile_len // STEP
     smem = pl.BlockSpec(memory_space=pltpu.SMEM)
     lengths = [len(g) * tile_count * NB * per_tile + 4 * BATCH for g in groups]
     return pl.pallas_call(
-        functools.partial(plan_kernel, groups, tile_count, per_tile),
+        functools.partial(plan_kernel, groups, tile_count, per_tile, slabs),
         out_shape=[jax.ShapeDtypeStruct((len(groups),), jnp.int32)]
         + [jax.ShapeDtypeStruct((n,), jnp.int32) for n in lengths],
         in_specs=[smem] * 3,
         out_specs=[smem] * (1 + len(groups)),
+        cost_estimate=pl.CostEstimate(flops=5_000_000_000, bytes_accessed=20_000, transcendentals=0),
         name="plan",
     )(info, counts, rows)
 
@@ -296,7 +299,7 @@
     else:
         block = jnp.stack([own, from_wall(own, 1), from_wall(own, -1)])
     near, far = around(block, -2), around(block, -4)
-    left = own_factors(own, weighted)
+    left = own_factors(own, weighted).reshape(tile_count * tile_len, -1)
     held = jnp.stack([block, near, far])
     other = exchange(held)
 
@@ -308,19 +311,18 @@
         head = [low_ok, one, high_ok, one, 0 * one, one, one, 2 - 2 * walled, 0 * one]
     else:
         head = [low_ok, one, high_ok, one, 0 * one, 2 * one, one, 0 * one, 2 * one]
-    near_at = 3 + odd
-    info = jnp.stack(head + [near_at, one, near_at + 1, 2 * one])
+    info = jnp.stack(head + [odd, one, odd + 1, 2 * one])
     rows = lists[0, 0].reshape(R + 1, tile_count * NB)
     totals, plan_same, plan_ahead = plans_of(
-        info, own_counts, rows, ((0,), (1, 2, 3, 4)), tile_len
+        info, own_counts, rows, ((0,), (1, 2, 3, 4)), tile_len, block.shape[0]
     )
     (gained_same,) = pairs(
-        jnp.stack(head + [0 * one]), totals, plan_same, left, [block[None]],
+        info, totals, plan_same, left, [block[None]],
         ((0.0, 0),), False, 0, "same",
     )
     gained_ahead, back = pairs(
-        info, totals, plan_ahead, left, [jnp.concatenate([held, other])],
-        ((1.0, 0), (2.0, 0), (3.0, 0), (4.0, 0)), True, 1, "ahead",
+        info, totals, plan_ahead, left, [held, other],
+        ((1.0, 1), (2.0, 0), (3.0, 1), (4.0, 0)), True, 1, "ahead",
     )
     back = back.reshape(R, -1, tile_len)
     back_odd, back_even = back[0::2], back[1::2]

time: 73 us -> 66.8 us (0.915)
  Pallas kernels: 37.3 us -> 33.2 us
  waiting for transfers between devices: 13.3 us -> 11 us
  other arithmetic: 4.09 us -> 2.95 us
  starting transfers between devices: 10.5 us -> 11.5 us
    pallas_call x2, Pallas kernels: 31.9 us -> 29 us  [pairs(): pl.pallas_call(functools.partial(pairs_kernel, offsets, tile_count, group...]
    ppermute x4, waiting for transfers between devices: 11.7 us -> 9.45 us  [around(): lax.ppermute(block, 'chan', [((i - distance) % size, i) for i in range(si...]
    convert_element_type x1 -> x0, local copies, waits for them, and re-layouts: 1.33 us -> none  [own_factors(): return jnp.swapaxes(stacked, 1, 2).astype(jnp.bfloat16)]
    reshape x0 -> x1, local copies, waits for them, and re-layouts: none -> 1.32 us  [on_device(): left = own_factors(own, weighted).reshape(tile_count * tile_len, -1)]
    pallas_call x1, Pallas kernels: 5.33 us -> 4.16 us  [plans_of(): pl.pallas_call(functools.partial(plan_kernel, groups, tile_count, per_til...]
    concatenate x1 -> x0, other arithmetic: 1.15 us -> none  [on_device(): jnp.concatenate([held, other])]
    ppermute x4, starting transfers between devices: 7.11 us -> 8.14 us  [around(): lax.ppermute(block, 'chan', [((i - distance) % size, i) for i in range(si...]
    unnamed x13 -> x17, local copies, waits for them, and re-layouts: 2.1 us -> 2.84 us
  transfers between devices with their start and end apart: 8 -> 8, of which waited for: 5 -> 6; matrix products, arithmetic and copies ran while one was open for 5% -> 5% of each run, Pallas kernels for 19% -> 18%
where the time goes in v3:
time: 66.8 us; the launch traced here: 66.1 us
  Pallas kernels  33.2 us (50%)
  starting transfers between devices  11.5 us (17%)
  waiting for transfers between devices  11 us (16%)
  local copies, waits for them, and re-layouts  7.19 us (11%)
  other arithmetic  2.95 us (4%)
    pallas_call x2, Pallas kernels, pairs(): pl.pallas_call(functools.partial(pairs_kernel, offsets, tile_count, group...  29 us
    ppermute x4, waiting for transfers between devices, around(): lax.ppermute(block, 'chan', [((i - distance) % size, i) for i in range(si...  9.45 us
    ppermute x4, starting transfers between devices, around(): lax.ppermute(block, 'chan', [((i - distance) % size, i) for i in range(si...  8.14 us
    pallas_call x1, Pallas kernels, plans_of(): pl.pallas_call(functools.partial(plan_kernel, groups, tile_count, per_til...  4.16 us
    ppermute x1, starting transfers between devices, on_device(): block = jnp.stack([own, lax.ppermute(own, 'wall', swap)])  3.03 us
    unnamed x17, local copies, waits for them, and re-layouts  2.84 us
  transfers between devices with their start and end apart: 8, of which 6 were waited for; matrix products, arithmetic and copies ran while one was open for 5% of the time, Pallas kernels for 18%

profile of v3, /device:TPU:0, one launch (start us, length us, event | category | flops | bytes accessed | tf_op | source)
XLA Modules:
  0.0 66.1 jit_solution(12197591092533319492)
XLA Ops:
  0.0 0.0 copy-start.5
  0.0 0.7 copy-done.5
  0.7 0.8 %compare_select_fusion = f32[16,1,256]{2,1,0:T(1,128)S(1)} fusion(f32[16,1,256]{2,1,0:T(1,128)} %bitcast.38, s32[16]{0:T(128)S(1)} %bitcast.40), kind=kLoop, calls=%fused_computation.10 | loop fusion | flops 8192 | bytes 32832 | tf_op jit(solution)/shard_map/mul | solution.py:292
  1.5 0.9 %reduce = f32[3,4096]{1,0:T(4,128)S(1)} reduce(f32[3,1,1,4096]{3,2,1,0:T(1,128)} %param.5, f32[]{:T(128)} %constant.53), dimensions={1,2}, to_apply=%param.5.reduce_sub_computation | reduce | bytes 98308 | tf_op args[0]
  2.4 3.0 %collective-permute-start = (f32[16,4,256]{2,1,0:T(4,128)S(1)}, f32[16,4,256]{2,1,0:T(4,128)S(1)}, u32[]{:S(2)}, u32[]{:S(2)}) collective-permute-start(f32[16,4,256]{2,1,0:T(4,128)S(1)} %pad_maximum_fusion.2), channel_id=1, source_target_pairs={{0,1},{1,0},{2,3},{3,2},{4,5},{5,4},{6,7},{7,6},{8,9},{9,8},{10,11... | collective-permute-start | bytes 196616 | tf_op jit(solution)/shard_map/ppermute | solution.py:298
  5.5 0.0 copy-start.4
  5.5 0.7 %copy-done.4 = s32[1,1,5,16,2]{3,4,2,1,0:T(2,128)S(1)} copy-done((s32[1,1,5,16,2]{3,4,2,1,0:T(2,128)S(1)}, s32[1,1,5,16,2]{3,4,2,1,0:T(2,128)}, u32[]{:S(2)}) %copy-start.4) | copy-done | bytes 664
  6.2 0.1 copy.7
  6.3 0.0 copy-start.7
  6.3 0.7 %copy.8.lists = s32[5,32]{1,0:T(8,128)} copy(s32[5,32]{0,1:T(8,128)S(1)} %bitcast.36) | data formatting | bytes 1280 | tf_op jit(solution)/shard_map/reshape;squeeze | solution.py:315
  6.9 0.0 copy-done.7
  6.9 0.1 multiply_reduce_fusion
  7.1 0.1 concatenate.10
  7.4 0.3 collective-permute-done
  7.8 0.0 copy-start.1
  7.8 5.1 %collective-permute-start.1 = (f32[2,16,4,256]{3,2,1,0:T(4,128)S(1)}, f32[2,16,4,256]{3,2,1,0:T(4,128)S(1)}, u32[]{:S(2)}, u32[]{:S(2)}) collective-permute-start(f32[2,16,4,256]{3,2,1,0:T(4,128)S(1)} %get-tuple-element.20), channel_id=1, source_target_pairs={{4,0},{6,2},{8,4},{10,6},{12,8},{14,10},{16,12},{18,14},{20,16},{2... | collective-permute-start | bytes 393224 | tf_op jit(solution)/shard_map/ppermute | solution.py:268
  12.9 0.4 collective-permute-start.2
  13.4 1.3 %copy.13 = bf16[16,256,48]{2,1,0:T(8,128)(2,1)} copy(bf16[16,256,48]{1,2,0:T(8,128)(2,1)S(1)} %bitcast.32) | data formatting | bytes 786432 | tf_op jit(solution)/shard_map/reshape | solution.py:302
  14.7 0.7 %stack.50.info = s32[13]{0:T(128)} concatenate(s32[1]{0:T(128)} %bitcast.1, s32[1]{0:T(128)} %constant.17.clone.1, s32[1]{0:T(128)} %bitcast.2, s32[1]{0:T(128)} %constant.17.clone.1, s32[1]{0:T(128)} %constant.38.clone.1, s32[2]{0:T(128)S(1)} %broadcast.44, s32[1]{0:T(128)} %bitcast.3, s32[1]{0:T(128)} %constant.38.clone.1, s32[1]{0:T(128)} %bitcast.4, s32[1]{0:T(128)} %constant.17.clone.1, ...), dimensions={0} | concatenate | bytes 104 | tf_op jit(solution)/shard_map/stack | solution.py:314
  15.4 0.6 collective-permute-done.1
  16.0 1.9 %collective-permute-done.2 = f32[2,16,4,256]{3,2,1,0:T(4,128)S(1)} collective-permute-done((f32[2,16,4,256]{3,2,1,0:T(4,128)S(1)}, f32[2,16,4,256]{3,2,1,0:T(4,128)S(1)}, u32[]{:S(2)}, u32[]{:S(2)}) %collective-permute-start.2) | collective-permute-done | bytes 131104 | tf_op jit(solution)/shard_map/ppermute | solution.py:268
  17.9 0.0 copy-done.1
  17.9 0.1 pad_maximum_fusion.refs_0_
  18.0 0.0 copy-start
  18.0 0.1 collective-permute-start.3
  18.1 4.2 %plan.1 = (s32[2]{0:T(128)}, s32[144]{0:T(256)}, s32[528]{0:T(1024)}) custom-call(s32[13]{0:T(128)} %stack.50.info, s32[16]{0:T(128)} %bitcast.39, s32[5,32]{1,0:T(8,128)} %copy.8.lists), custom_call_target="tpu_custom_call" | custom-call | flops 5000000000 | bytes 20000 | tf_op jit(solution)/shard_map/plan/pallas_call | solution.py:252
  22.2 0.0 copy-done
  22.3 0.0 collective-permute-done.3.refs_1_
  22.3 0.0 copy-start.2
  22.3 0.7 %copy-done.2 = f32[3,2,16,4,256]{4,3,2,1,0:T(4,128)} copy-done((f32[3,2,16,4,256]{4,3,2,1,0:T(4,128)}, f32[3,2,16,4,256]{4,3,2,1,0:T(4,128)S(1)}, u32[]{:S(2)}) %copy-start.2) | copy-done | bytes 393240
  23.0 21.4 %ahead.1 = (f32[16,256]{1,0:T(8,128)}, f32[128,256]{1,0:T(8,128)}) custom-call(s32[13]{0:T(128)} %stack.50.info, s32[2]{0:T(128)} %get-tuple-element.10.totals, s32[528]{0:T(1024)} %get-tuple-element.12.plan, bf16[4096,48]{1,0:T(8,128)(2,1)} %bitcast.27, f32[3,2,16,4,256]{4,3,2,1,0:T(4,128)} %copy-done, f32[3,2,16,4,256]{4,3,2,1,0:T(4,128)} %copy-done.2), custom_call_target="tpu_custom_call" | custom-call | tf_op jit(solution)/shard_map/ahead/pallas_call | solution.py:234
  44.4 0.9 %fusion.8 = (f32[2,32,256]{2,1,0:T(8,128)S(1)}, f32[2,32,256]{2,1,0:T(8,128)S(1)}) fusion(f32[4,32,256]{2,1,0:T(8,128)} %bitcast.33), kind=kLoop, calls=%fused_computation.28 | loop fusion | bytes 262144 | tf_op jit(solution)/shard_map/slice | solution.py:328
  45.3 0.1 collective-permute-start.4
  45.4 1.2 %collective-permute-done.4 = f32[2,32,256]{2,1,0:T(8,128)S(1)} collective-permute-done((f32[2,32,256]{2,1,0:T(8,128)S(1)}, f32[2,32,256]{2,1,0:T(8,128)S(1)}, u32[]{:S(2)}, u32[]{:S(2)}) %collective-permute-start.4) | collective-permute-done | bytes 65568 | tf_op jit(solution)/shard_map/ppermute | solution.py:273
  46.6 0.1 collective-permute-start.5
  46.7 2.5 %collective-permute-start.6 = (f32[32,256]{1,0:T(8,128)S(1)}, f32[32,256]{1,0:T(8,128)S(1)}, u32[]{:S(2)}, u32[]{:S(2)}) collective-permute-start(f32[32,256]{1,0:T(8,128)S(1)} %get-tuple-element.15), channel_id=1, source_target_pairs={{24,0},{26,2},{28,4},{30,6},{0,8},{2,10},{4,12},{6,14},{8,16},{10,... | collective-permute-start | bytes 98312 | tf_op jit(solution)/shard_map/ppermute | solution.py:268
  49.2 4.1 %collective-permute-done.5 = f32[32,256]{1,0:T(8,128)S(1)} collective-permute-done((f32[32,256]{1,0:T(8,128)S(1)}, f32[32,256]{1,0:T(8,128)S(1)}, u32[]{:S(2)}, u32[]{:S(2)}) %collective-permute-start.5) | collective-permute-done | bytes 32800 | tf_op jit(solution)/shard_map/ppermute | solution.py:268
  53.3 2.9 %collective-permute-done.6 = f32[32,256]{1,0:T(8,128)S(1)} collective-permute-done((f32[32,256]{1,0:T(8,128)S(1)}, f32[32,256]{1,0:T(8,128)S(1)}, u32[]{:S(2)}, u32[]{:S(2)}) %collective-permute-start.6) | collective-permute-done | bytes 32800 | tf_op jit(solution)/shard_map/ppermute | solution.py:268
  56.1 0.2 collective-permute-start.7
  56.4 0.0 copy-start.3
  56.4 7.6 %same.1 = f32[16,256]{1,0:T(8,128)} custom-call(s32[13]{0:T(128)} %stack.50.info, s32[2]{0:T(128)} %get-tuple-element.10.totals, s32[144]{0:T(256)} %get-tuple-element.11.plan, bf16[4096,48]{1,0:T(8,128)(2,1)} %bitcast.28, f32[1,2,16,4,256]{4,3,2,1,0:T(4,128)} %copy-done.1), custom_call_target="tpu_custom_call" | custom-call | tf_op jit(solution)/shard_map/same/pallas_call | solution.py:234
  64.0 0.0 copy-start.6
  64.0 0.0 collective-permute-done.7
  64.0 0.0 copy-done.3
  64.0 0.6 copy-done.6
  64.6 0.8 %fusion.6 = f32[16,256]{1,0:T(8,128)S(1)} fusion(f32[16,256]{1,0:T(8,128)S(1)} %collective-permute-done.7, f32[32,256]{1,0:T(8,128)S(1)} %bitcast_add_fusion, f32[16,256]{1,0:T(8,128)} %same.1, f32[16,256]{1,0:T(8,128)S(1)} %copy-done.3, s32[16]{0:T(128)S(1)} %bitcast.41), kind=kLoop, calls=%fused_computation.20 | loop fusion | flops 24576 | bytes 81984 | tf_op jit(solution)/shard_map/mul | solution.py:341
  65.4 0.6 reshape.84
  (16 shorter events, 0.3 us)
Async XLA Ops:
  0.0 0.7 copy-start.5
  2.4 5.3 %collective-permute-start = (f32[16,4,256]{2,1,0:T(4,128)S(1)}, f32[16,4,256]{2,1,0:T(4,128)S(1)}, u32[]{:S(2)}, u32[]{:S(2)}) collective-permute-start(f32[16,4,256]{2,1,0:T(4,128)S(1)} %pad_maximum_fusion.2), channel_id=1, source_target_pairs={{0,1},{1,0},{2,3},{3,2},{4,5},{5,4},{6,7},{7,6},{8,9},{9,8},{10,11... | collective-permute-start | bytes 196616 | tf_op jit(solution)/shard_map/ppermute | solution.py:298
  5.5 0.7 %copy-start.4 = (s32[1,1,5,16,2]{3,4,2,1,0:T(2,128)S(1)}, s32[1,1,5,16,2]{3,4,2,1,0:T(2,128)}, u32[]{:S(2)}) copy-start(s32[1,1,5,16,2]{3,4,2,1,0:T(2,128)} %param.8) | copy-start | bytes 1924
  6.3 0.7 %copy-start.7 = (f32[3]{0:T(128)S(1)}, f32[3]{0:T(128)}, u32[]{:S(2)}) copy-start(f32[3]{0:T(128)} %constant.52) | copy-start | bytes 40
  7.8 10.1 %copy-start.1 = (f32[1,2,16,4,256]{4,3,2,1,0:T(4,128)}, f32[1,2,16,4,256]{4,3,2,1,0:T(4,128)S(1)}, u32[]{:S(2)}) copy-start(f32[1,2,16,4,256]{4,3,2,1,0:T(4,128)S(1)} %get-tuple-element.19.refs_0_) | copy-start | bytes 393220
  7.8 8.2 %collective-permute-start.1 = (f32[2,16,4,256]{3,2,1,0:T(4,128)S(1)}, f32[2,16,4,256]{3,2,1,0:T(4,128)S(1)}, u32[]{:S(2)}, u32[]{:S(2)}) collective-permute-start(f32[2,16,4,256]{3,2,1,0:T(4,128)S(1)} %get-tuple-element.20), channel_id=1, source_target_pairs={{4,0},{6,2},{8,4},{10,6},{12,8},{14,10},{16,12},{18,14},{20,16},{2... | collective-permute-start | bytes 393224 | tf_op jit(solution)/shard_map/ppermute | solution.py:268
  12.9 5.0 %collective-permute-start.2 = (f32[2,16,4,256]{3,2,1,0:T(4,128)S(1)}, f32[2,16,4,256]{3,2,1,0:T(4,128)S(1)}, u32[]{:S(2)}, u32[]{:S(2)}) collective-permute-start(f32[2,16,4,256]{3,2,1,0:T(4,128)S(1)} %get-tuple-element.20), channel_id=1, source_target_pairs={{8,0},{10,2},{12,4},{14,6},{16,8},{18,10},{20,12},{22,14},{24,16},... | collective-permute-start | bytes 393224 | tf_op jit(solution)/shard_map/ppermute | solution.py:268
  18.0 4.3 %copy-start = (f32[3,2,16,4,256]{4,3,2,1,0:T(4,128)}, f32[3,2,16,4,256]{4,3,2,1,0:T(4,128)S(1)}, u32[]{:S(2)}) copy-start(f32[3,2,16,4,256]{4,3,2,1,0:T(4,128)S(1)} %pad_maximum_fusion.refs_0_) | copy-start | bytes 1179652
  18.0 4.3 %collective-permute-start.3 = (f32[3,2,16,4,256]{4,3,2,1,0:T(4,128)S(1)}, f32[3,2,16,4,256]{4,3,2,1,0:T(4,128)S(1)}, u32[]{:S(2)}, u32[]{:S(2)}) collective-permute-start(f32[3,2,16,4,256]{4,3,2,1,0:T(4,128)S(1)} %pad_maximum_fusion.refs_0_), channel_id=1, source_target_pairs={{2,0},{0,2},{6,4},{4,6},{10,8},{8,10},{14,12},{12,14},{18,16},{16,... | collective-permute-start | bytes 1179656 | tf_op jit(solution)/shard_map/ppermute | solution.py:273
  22.3 0.8 %copy-start.2 = (f32[3,2,16,4,256]{4,3,2,1,0:T(4,128)}, f32[3,2,16,4,256]{4,3,2,1,0:T(4,128)S(1)}, u32[]{:S(2)}) copy-start(f32[3,2,16,4,256]{4,3,2,1,0:T(4,128)S(1)} %collective-permute-done.3.refs_1_) | copy-start | bytes 1179652
  45.3 1.3 %collective-permute-start.4 = (f32[2,32,256]{2,1,0:T(8,128)S(1)}, f32[2,32,256]{2,1,0:T(8,128)S(1)}, u32[]{:S(2)}, u32[]{:S(2)}) collective-permute-start(f32[2,32,256]{2,1,0:T(8,128)S(1)} %get-tuple-element.17), channel_id=1, source_target_pairs={{2,0},{0,2},{6,4},{4,6},{10,8},{8,10},{14,12},{12,14},{18,16},{16,... | collective-permute-start | bytes 196616 | tf_op jit(solution)/shard_map/ppermute | solution.py:273
  46.6 6.7 %collective-permute-start.5 = (f32[32,256]{1,0:T(8,128)S(1)}, f32[32,256]{1,0:T(8,128)S(1)}, u32[]{:S(2)}, u32[]{:S(2)}) collective-permute-start(f32[32,256]{1,0:T(8,128)S(1)} %get-tuple-element.16), channel_id=1, source_target_pairs={{28,0},{30,2},{0,4},{2,6},{4,8},{6,10},{8,12},{10,14},{12,16},{14,... | collective-permute-start | bytes 98312 | tf_op jit(solution)/shard_map/ppermute | solution.py:268
  46.7 9.4 %collective-permute-start.6 = (f32[32,256]{1,0:T(8,128)S(1)}, f32[32,256]{1,0:T(8,128)S(1)}, u32[]{:S(2)}, u32[]{:S(2)}) collective-permute-start(f32[32,256]{1,0:T(8,128)S(1)} %get-tuple-element.15), channel_id=1, source_target_pairs={{24,0},{26,2},{28,4},{30,6},{0,8},{2,10},{4,12},{6,14},{8,16},{10,... | collective-permute-start | bytes 98312 | tf_op jit(solution)/shard_map/ppermute | solution.py:268
  56.1 7.8 %collective-permute-start.7 = (f32[16,256]{1,0:T(8,128)S(1)}, f32[16,256]{1,0:T(8,128)S(1)}, u32[]{:S(2)}, u32[]{:S(2)}) collective-permute-start(f32[16,256]{1,0:T(8,128)S(1)} %slice.41), channel_id=1, source_target_pairs={{0,1},{1,0},{2,3},{3,2},{4,5},{5,4},{6,7},{7,6},{8,9},{9,8},{10,11... | collective-permute-start | bytes 49160 | tf_op jit(solution)/shard_map/ppermute | solution.py:338
  56.4 7.6 %copy-start.3 = (f32[16,256]{1,0:T(8,128)S(1)}, f32[16,256]{1,0:T(8,128)}, u32[]{:S(2)}) copy-start(f32[16,256]{1,0:T(8,128)} %get-tuple-element.13) | copy-start | bytes 49156
  64.0 0.7 copy-start.6

commit v4 on v3

--- a/solution.py
+++ b/solution.py
@@ -12,7 +12,7 @@
 R = 4
 LANES = 128
 STEP = 64
-BATCH = 4
+BATCH = 8
 EPS = 0.0001 / (R * R)
 
 
@@ -301,7 +301,6 @@
     near, far = around(block, -2), around(block, -4)
     left = own_factors(own, weighted).reshape(tile_count * tile_len, -1)
     held = jnp.stack([block, near, far])
-    other = exchange(held)
 
     low_ok = (wall > 0).astype(jnp.int32)
     high_ok = (wall < walls - 1).astype(jnp.int32)
@@ -313,9 +312,12 @@
         head = [low_ok, one, high_ok, one, 0 * one, 2 * one, one, 0 * one, 2 * one]
     info = jnp.stack(head + [odd, one, odd + 1, 2 * one])
     rows = lists[0, 0].reshape(R + 1, tile_count * NB)
+    rows, block = lax.optimization_barrier((rows, block))
     totals, plan_same, plan_ahead = plans_of(
         info, own_counts, rows, ((0,), (1, 2, 3, 4)), tile_len, block.shape[0]
     )
+    held, totals, plan_ahead, left = lax.optimization_barrier((held, totals, plan_ahead, left))
+    other = exchange(held)
     (gained_same,) = pairs(
         info, totals, plan_same, left, [block[None]],
         ((0.0, 0),), False, 0, "same",

time: 66.8 us -> 61.9 us (0.927)
  waiting for transfers between devices: 11 us -> 7.22 us
  Pallas kernels: 33.2 us -> 31.1 us
    ppermute x4, waiting for transfers between devices: 9.45 us -> 5.69 us  [around(): lax.ppermute(block, 'chan', [((i - distance) % size, i) for i in range(si...]
    pallas_call x2, Pallas kernels: 29 us -> 27 us  [pairs(): pl.pallas_call(functools.partial(pairs_kernel, offsets, tile_count, group...]
    optimization_barrier x0 -> x2, local copies, waits for them, and re-layouts: none -> 1.99 us  [the longest x1 1.32 us: on_device(): lax.optimization_barrier((held, totals, plan_ahead, left))]
    reshape x1, local copies, waits for them, and re-layouts: 1.32 us -> 0.03 us  [on_device(): left = own_factors(own, weighted).reshape(tile_count * tile_len, -1)]
    ppermute x4, starting transfers between devices: 8.14 us -> 6.99 us  [around(): lax.ppermute(block, 'chan', [((i - distance) % size, i) for i in range(si...]
    ppermute x1, starting transfers between devices: 0.21 us -> 1.31 us  [on_device(): total = total + lax.ppermute(returns[1], 'wall', swap)]
  transfers between devices with their start and end apart: 8 -> 8, of which waited for: 6 -> 4; matrix products, arithmetic and copies ran while one was open for 5% -> 5% of each run, Pallas kernels for 18% -> 18%
where the time goes in v4:
time: 61.9 us; the launch traced here: 60.9 us
  Pallas kernels  31.1 us (50%)
  starting transfers between devices  11.6 us (19%)
  local copies, waits for them, and re-layouts  7.79 us (13%)
  waiting for transfers between devices  7.22 us (12%)
  other arithmetic  2.95 us (5%)
    pallas_call x2, Pallas kernels, pairs(): pl.pallas_call(functools.partial(pairs_kernel, offsets, tile_count, group...  27 us
    ppermute x4, starting transfers between devices, around(): lax.ppermute(block, 'chan', [((i - distance) % size, i) for i in range(si...  6.99 us
    ppermute x4, waiting for transfers between devices, around(): lax.ppermute(block, 'chan', [((i - distance) % size, i) for i in range(si...  5.69 us
    pallas_call x1, Pallas kernels, plans_of(): pl.pallas_call(functools.partial(plan_kernel, groups, tile_count, per_til...  4.17 us
    unnamed x17, local copies, waits for them, and re-layouts  3.41 us
    ppermute x1, starting transfers between devices, on_device(): block = jnp.stack([own, lax.ppermute(own, 'wall', swap)])  3.03 us
    ppermute x2, waiting for transfers between devices, exchange(): return lax.ppermute(block, 'chan', [(i ^ 1, i) for i in range(size)])  1.53 us
    optimization_barrier x1, local copies, waits for them, and re-layouts, on_device(): lax.optimization_barrier((held, totals, plan_ahead, left))  1.32 us
  transfers between devices with their start and end apart: 8, of which 4 were waited for; matrix products, arithmetic and copies ran while one was open for 5% of the time, Pallas kernels for 18%

profile of v4, /device:TPU:0, one launch (start us, length us, event | category | flops | bytes accessed | tf_op | source)
XLA Modules:
  0.0 60.9 jit_solution(15470612286602944214)
XLA Ops:
  0.0 0.0 copy-start.5
  0.0 0.7 %copy-done.5 = s32[1,1,16]{2,1,0:T(1,128)S(1)} copy-done((s32[1,1,16]{2,1,0:T(1,128)S(1)}, s32[1,1,16]{2,1,0:T(1,128)}, u32[]{:S(2)}) %copy-start.5) | copy-done | bytes 88
  0.7 0.8 %compare_select_fusion = f32[16,1,256]{2,1,0:T(1,128)S(1)} fusion(f32[16,1,256]{2,1,0:T(1,128)} %bitcast.40, s32[16]{0:T(128)S(1)} %bitcast.42), kind=kLoop, calls=%fused_computation.10 | loop fusion | flops 8192 | bytes 32832 | tf_op jit(solution)/shard_map/mul | solution.py:292
  1.5 0.9 %reduce = f32[3,4096]{1,0:T(4,128)S(1)} reduce(f32[3,1,1,4096]{3,2,1,0:T(1,128)} %param.5, f32[]{:T(128)} %constant.53), dimensions={1,2}, to_apply=%param.5.reduce_sub_computation | reduce | bytes 98308 | tf_op args[0]
  2.4 3.0 %collective-permute-start = (f32[16,4,256]{2,1,0:T(4,128)S(1)}, f32[16,4,256]{2,1,0:T(4,128)S(1)}, u32[]{:S(2)}, u32[]{:S(2)}) collective-permute-start(f32[16,4,256]{2,1,0:T(4,128)S(1)} %pad_maximum_fusion.2), channel_id=1, source_target_pairs={{0,1},{1,0},{2,3},{3,2},{4,5},{5,4},{6,7},{7,6},{8,9},{9,8},{10,11... | collective-permute-start | bytes 196616 | tf_op jit(solution)/shard_map/ppermute | solution.py:298
  5.5 0.0 copy-start.4
  5.5 0.7 %copy-done.4 = s32[1,1,5,16,2]{3,4,2,1,0:T(2,128)S(1)} copy-done((s32[1,1,5,16,2]{3,4,2,1,0:T(2,128)S(1)}, s32[1,1,5,16,2]{3,4,2,1,0:T(2,128)}, u32[]{:S(2)}) %copy-start.4) | copy-done | bytes 664
  6.2 0.0 copy-start.7
  6.2 0.1 copy.8
  6.3 0.6 copy-done.7
  6.8 0.1 multiply_reduce_fusion
  7.0 0.1 concatenate.11
  7.3 0.7 %stack.52.info = s32[13]{0:T(128)} concatenate(s32[1]{0:T(128)} %bitcast.1, s32[1]{0:T(128)} %constant.17.clone.1, s32[1]{0:T(128)} %bitcast.2, s32[1]{0:T(128)} %constant.17.clone.1, s32[1]{0:T(128)} %constant.38.clone.1, s32[2]{0:T(128)S(1)} %broadcast.44, s32[1]{0:T(128)} %bitcast.3, s32[1]{0:T(128)} %constant.38.clone.1, s32[1]{0:T(128)} %bitcast.4, s32[1]{0:T(128)} %constant.17.clone.1, ...), dimensions={0} | concatenate | bytes 104 | tf_op jit(solution)/shard_map/stack | solution.py:313
  8.0 0.0 collective-permute-done
  8.1 0.0 copy-start.1
  8.1 4.8 %collective-permute-start.1 = (f32[2,16,4,256]{3,2,1,0:T(4,128)S(1)}, f32[2,16,4,256]{3,2,1,0:T(4,128)S(1)}, u32[]{:S(2)}, u32[]{:S(2)}) collective-permute-start(f32[2,16,4,256]{3,2,1,0:T(4,128)S(1)} %get-tuple-element.22), channel_id=1, source_target_pairs={{4,0},{6,2},{8,4},{10,6},{12,8},{14,10},{16,12},{18,14},{20,16},{2... | collective-permute-start | bytes 393224 | tf_op jit(solution)/shard_map/ppermute | solution.py:268
  12.9 0.4 collective-permute-start.2
  13.4 0.7 %copy.9.lists = s32[5,32]{1,0:T(8,128)} copy(s32[5,32]{0,1:T(8,128)S(1)} %bitcast.38) | data formatting | bytes 1280 | tf_op jit(solution)/shard_map/optimization_barrier | solution.py:315
  14.0 4.2 %plan.1 = (s32[2]{0:T(128)}, s32[160]{0:T(256)}, s32[544]{0:T(1024)}) custom-call(s32[13]{0:T(128)} %stack.52.info, s32[16]{0:T(128)} %bitcast.41, s32[5,32]{1,0:T(8,128)} %copy.9.lists), custom_call_target="tpu_custom_call" | custom-call | flops 5000000000 | bytes 20000 | tf_op jit(solution)/shard_map/plan/pallas_call | solution.py:252
  18.2 0.0 copy-done.1
  18.2 0.0 collective-permute-done.1
  18.2 0.0 collective-permute-done.2
  18.2 0.1 pad_maximum_fusion.refs_0_
  18.3 0.0 copy-start
  18.3 0.1 collective-permute-start.3
  18.4 1.3 %copy.11.left_ref = bf16[4096,48]{1,0:T(8,128)(2,1)} copy(bf16[4096,48]{0,1:T(8,128)(2,1)S(1)} %bitcast.29) | data formatting | bytes 786432 | tf_op jit(solution)/shard_map/optimization_barrier | solution.py:319
  19.7 0.0 copy-done
  19.8 0.4 collective-permute-done.3.refs_1_
  20.1 0.0 copy-start.2
  20.1 0.8 %copy-done.2 = f32[3,2,16,4,256]{4,3,2,1,0:T(4,128)} copy-done((f32[3,2,16,4,256]{4,3,2,1,0:T(4,128)}, f32[3,2,16,4,256]{4,3,2,1,0:T(4,128)S(1)}, u32[]{:S(2)}) %copy-start.2) | copy-done | bytes 393240
  20.9 20.4 %ahead.1 = (f32[16,256]{1,0:T(8,128)}, f32[128,256]{1,0:T(8,128)}) custom-call(s32[13]{0:T(128)} %stack.52.info, s32[2]{0:T(128)} %get-tuple-element.19.totals, s32[544]{0:T(1024)} %get-tuple-element.23.plan, bf16[4096,48]{1,0:T(8,128)(2,1)} %copy.11.left_ref, f32[3,2,16,4,256]{4,3,2,1,0:T(4,128)} %copy-done, f32[3,2,16,4,256]{4,3,2,1,0:T(4,128)} %copy-done.2), custom_call_target="tpu_custom_call" | custom-call | tf_op jit(solution)/shard_map/ahead/pallas_call | solution.py:234
  41.3 0.9 %fusion.8 = (f32[2,32,256]{2,1,0:T(8,128)S(1)}, f32[2,32,256]{2,1,0:T(8,128)S(1)}) fusion(f32[4,32,256]{2,1,0:T(8,128)} %bitcast.35), kind=kLoop, calls=%fused_computation.28 | loop fusion | bytes 262144 | tf_op jit(solution)/shard_map/slice | solution.py:330
  42.2 0.2 collective-permute-start.4
  42.4 1.1 %collective-permute-done.4 = f32[2,32,256]{2,1,0:T(8,128)S(1)} collective-permute-done((f32[2,32,256]{2,1,0:T(8,128)S(1)}, f32[2,32,256]{2,1,0:T(8,128)S(1)}, u32[]{:S(2)}, u32[]{:S(2)}) %collective-permute-start.4) | collective-permute-done | bytes 65568 | tf_op jit(solution)/shard_map/ppermute | solution.py:273
  43.6 0.4 collective-permute-start.5
  44.0 1.3 %collective-permute-start.6 = (f32[32,256]{1,0:T(8,128)S(1)}, f32[32,256]{1,0:T(8,128)S(1)}, u32[]{:S(2)}, u32[]{:S(2)}) collective-permute-start(f32[32,256]{1,0:T(8,128)S(1)} %get-tuple-element.27), channel_id=1, source_target_pairs={{24,0},{26,2},{28,4},{30,6},{0,8},{2,10},{4,12},{6,14},{8,16},{10,... | collective-permute-start | bytes 98312 | tf_op jit(solution)/shard_map/ppermute | solution.py:268
  45.3 4.9 %collective-permute-done.5 = f32[32,256]{1,0:T(8,128)S(1)} collective-permute-done((f32[32,256]{1,0:T(8,128)S(1)}, f32[32,256]{1,0:T(8,128)S(1)}, u32[]{:S(2)}, u32[]{:S(2)}) %collective-permute-start.5) | collective-permute-done | bytes 32800 | tf_op jit(solution)/shard_map/ppermute | solution.py:268
  50.2 0.8 %collective-permute-done.6 = f32[32,256]{1,0:T(8,128)S(1)} collective-permute-done((f32[32,256]{1,0:T(8,128)S(1)}, f32[32,256]{1,0:T(8,128)S(1)}, u32[]{:S(2)}, u32[]{:S(2)}) %collective-permute-start.6) | collective-permute-done | bytes 32800 | tf_op jit(solution)/shard_map/ppermute | solution.py:268
  51.0 1.3 %collective-permute-start.7 = (f32[16,256]{1,0:T(8,128)S(1)}, f32[16,256]{1,0:T(8,128)S(1)}, u32[]{:S(2)}, u32[]{:S(2)}) collective-permute-start(f32[16,256]{1,0:T(8,128)S(1)} %slice.41), channel_id=1, source_target_pairs={{0,1},{1,0},{2,3},{3,2},{4,5},{5,4},{6,7},{7,6},{8,9},{9,8},{10,11... | collective-permute-start | bytes 49160 | tf_op jit(solution)/shard_map/ppermute | solution.py:340
  52.3 0.0 copy-start.3
  52.3 6.5 %same.1 = f32[16,256]{1,0:T(8,128)} custom-call(s32[13]{0:T(128)} %stack.52.info, s32[2]{0:T(128)} %get-tuple-element.19.totals, s32[160]{0:T(256)} %get-tuple-element.20.plan, bf16[4096,48]{1,0:T(8,128)(2,1)} %copy.11.left_ref, f32[1,2,16,4,256]{4,3,2,1,0:T(4,128)} %bitcast.34), custom_call_target="tpu_custom_call" | custom-call | tf_op jit(solution)/shard_map/same/pallas_call | solution.py:234
  58.8 0.0 copy-start.6
  58.8 0.0 collective-permute-done.7
  58.8 0.0 copy-done.3
  58.8 0.6 %copy-done.6 = s32[1,1,16]{2,1,0:T(1,128)S(1)} copy-done((s32[1,1,16]{2,1,0:T(1,128)S(1)}, s32[1,1,16]{2,1,0:T(1,128)}, u32[]{:S(2)}) %copy-start.6) | copy-done | bytes 88
  59.5 0.8 %fusion.6 = f32[16,256]{1,0:T(8,128)S(1)} fusion(f32[16,256]{1,0:T(8,128)S(1)} %collective-permute-done.7, f32[32,256]{1,0:T(8,128)S(1)} %bitcast_add_fusion, f32[16,256]{1,0:T(8,128)} %same.1, f32[16,256]{1,0:T(8,128)S(1)} %copy-done.3, s32[16]{0:T(128)S(1)} %bitcast.43), kind=kLoop, calls=%fused_computation.20 | loop fusion | flops 24576 | bytes 81984 | tf_op jit(solution)/shard_map/mul | solution.py:343
  60.3 0.6 %reshape.84 = f32[1,1,4096]{2,1,0:T(1,128)} reshape(f32[16,256]{1,0:T(8,128)S(1)} %fusion.6) | data formatting | bytes 32768 | tf_op jit(solution)/shard_map/reshape | solution.py:343
  (17 shorter events, 0.3 us)
Async XLA Ops:
  0.0 0.7 %copy-start.5 = (s32[1,1,16]{2,1,0:T(1,128)S(1)}, s32[1,1,16]{2,1,0:T(1,128)}, u32[]{:S(2)}) copy-start(s32[1,1,16]{2,1,0:T(1,128)} %param.7) | copy-start | bytes 196
  2.4 5.6 %collective-permute-start = (f32[16,4,256]{2,1,0:T(4,128)S(1)}, f32[16,4,256]{2,1,0:T(4,128)S(1)}, u32[]{:S(2)}, u32[]{:S(2)}) collective-permute-start(f32[16,4,256]{2,1,0:T(4,128)S(1)} %pad_maximum_fusion.2), channel_id=1, source_target_pairs={{0,1},{1,0},{2,3},{3,2},{4,5},{5,4},{6,7},{7,6},{8,9},{9,8},{10,11... | collective-permute-start | bytes 196616 | tf_op jit(solution)/shard_map/ppermute | solution.py:298
  5.5 0.7 %copy-start.4 = (s32[1,1,5,16,2]{3,4,2,1,0:T(2,128)S(1)}, s32[1,1,5,16,2]{3,4,2,1,0:T(2,128)}, u32[]{:S(2)}) copy-start(s32[1,1,5,16,2]{3,4,2,1,0:T(2,128)} %param.8) | copy-start | bytes 1924
  6.2 0.7 %copy-start.7 = (f32[3]{0:T(128)S(1)}, f32[3]{0:T(128)}, u32[]{:S(2)}) copy-start(f32[3]{0:T(128)} %constant.52) | copy-start | bytes 40
  8.1 10.1 %copy-start.1 = (f32[2,16,4,256]{3,2,1,0:T(4,128)}, f32[2,16,4,256]{3,2,1,0:T(4,128)S(1)}, u32[]{:S(2)}) copy-start(f32[2,16,4,256]{3,2,1,0:T(4,128)S(1)} %get-tuple-element.22) | copy-start | bytes 393220
  8.1 10.1 %collective-permute-start.1 = (f32[2,16,4,256]{3,2,1,0:T(4,128)S(1)}, f32[2,16,4,256]{3,2,1,0:T(4,128)S(1)}, u32[]{:S(2)}, u32[]{:S(2)}) collective-permute-start(f32[2,16,4,256]{3,2,1,0:T(4,128)S(1)} %get-tuple-element.22), channel_id=1, source_target_pairs={{4,0},{6,2},{8,4},{10,6},{12,8},{14,10},{16,12},{18,14},{20,16},{2... | collective-permute-start | bytes 393224 | tf_op jit(solution)/shard_map/ppermute | solution.py:268
  12.9 5.3 %collective-permute-start.2 = (f32[2,16,4,256]{3,2,1,0:T(4,128)S(1)}, f32[2,16,4,256]{3,2,1,0:T(4,128)S(1)}, u32[]{:S(2)}, u32[]{:S(2)}) collective-permute-start(f32[2,16,4,256]{3,2,1,0:T(4,128)S(1)} %get-tuple-element.22), channel_id=1, source_target_pairs={{8,0},{10,2},{12,4},{14,6},{16,8},{18,10},{20,12},{22,14},{24,16},... | collective-permute-start | bytes 393224 | tf_op jit(solution)/shard_map/ppermute | solution.py:268
  18.3 1.4 %copy-start = (f32[3,2,16,4,256]{4,3,2,1,0:T(4,128)}, f32[3,2,16,4,256]{4,3,2,1,0:T(4,128)S(1)}, u32[]{:S(2)}) copy-start(f32[3,2,16,4,256]{4,3,2,1,0:T(4,128)S(1)} %pad_maximum_fusion.refs_0_) | copy-start | bytes 1179652
  18.3 1.8 %collective-permute-start.3 = (f32[3,2,16,4,256]{4,3,2,1,0:T(4,128)S(1)}, f32[3,2,16,4,256]{4,3,2,1,0:T(4,128)S(1)}, u32[]{:S(2)}, u32[]{:S(2)}) collective-permute-start(f32[3,2,16,4,256]{4,3,2,1,0:T(4,128)S(1)} %pad_maximum_fusion.refs_0_), channel_id=1, source_target_pairs={{2,0},{0,2},{6,4},{4,6},{10,8},{8,10},{14,12},{12,14},{18,16},{16,... | collective-permute-start | bytes 1179656 | tf_op jit(solution)/shard_map/ppermute | solution.py:273
  20.1 0.8 %copy-start.2 = (f32[3,2,16,4,256]{4,3,2,1,0:T(4,128)}, f32[3,2,16,4,256]{4,3,2,1,0:T(4,128)S(1)}, u32[]{:S(2)}) copy-start(f32[3,2,16,4,256]{4,3,2,1,0:T(4,128)S(1)} %collective-permute-done.3.refs_1_) | copy-start | bytes 1179652
  42.2 1.3 %collective-permute-start.4 = (f32[2,32,256]{2,1,0:T(8,128)S(1)}, f32[2,32,256]{2,1,0:T(8,128)S(1)}, u32[]{:S(2)}, u32[]{:S(2)}) collective-permute-start(f32[2,32,256]{2,1,0:T(8,128)S(1)} %get-tuple-element.29), channel_id=1, source_target_pairs={{2,0},{0,2},{6,4},{4,6},{10,8},{8,10},{14,12},{12,14},{18,16},{16,... | collective-permute-start | bytes 196616 | tf_op jit(solution)/shard_map/ppermute | solution.py:273
  43.6 6.7 %collective-permute-start.5 = (f32[32,256]{1,0:T(8,128)S(1)}, f32[32,256]{1,0:T(8,128)S(1)}, u32[]{:S(2)}, u32[]{:S(2)}) collective-permute-start(f32[32,256]{1,0:T(8,128)S(1)} %get-tuple-element.28), channel_id=1, source_target_pairs={{28,0},{30,2},{0,4},{2,6},{4,8},{6,10},{8,12},{10,14},{12,16},{14,... | collective-permute-start | bytes 98312 | tf_op jit(solution)/shard_map/ppermute | solution.py:268
  44.0 7.0 %collective-permute-start.6 = (f32[32,256]{1,0:T(8,128)S(1)}, f32[32,256]{1,0:T(8,128)S(1)}, u32[]{:S(2)}, u32[]{:S(2)}) collective-permute-start(f32[32,256]{1,0:T(8,128)S(1)} %get-tuple-element.27), channel_id=1, source_target_pairs={{24,0},{26,2},{28,4},{30,6},{0,8},{2,10},{4,12},{6,14},{8,16},{10,... | collective-permute-start | bytes 98312 | tf_op jit(solution)/shard_map/ppermute | solution.py:268
  51.0 7.8 %collective-permute-start.7 = (f32[16,256]{1,0:T(8,128)S(1)}, f32[16,256]{1,0:T(8,128)S(1)}, u32[]{:S(2)}, u32[]{:S(2)}) collective-permute-start(f32[16,256]{1,0:T(8,128)S(1)} %slice.41), channel_id=1, source_target_pairs={{0,1},{1,0},{2,3},{3,2},{4,5},{5,4},{6,7},{7,6},{8,9},{9,8},{10,11... | collective-permute-start | bytes 49160 | tf_op jit(solution)/shard_map/ppermute | solution.py:340
  52.3 6.5 %copy-start.3 = (f32[16,256]{1,0:T(8,128)S(1)}, f32[16,256]{1,0:T(8,128)}, u32[]{:S(2)}) copy-start(f32[16,256]{1,0:T(8,128)} %get-tuple-element.25) | copy-start | bytes 49156
  58.8 0.7 %copy-start.6 = (s32[1,1,16]{2,1,0:T(1,128)S(1)}, s32[1,1,16]{2,1,0:T(1,128)}, u32[]{:S(2)}) copy-start(s32[1,1,16]{2,1,0:T(1,128)} %param.7) | copy-start | bytes 196
